TPU v7x, 32 devices: a 4x4x1 block of a 4x4x8 slice. The times are simulated.
32 devices in a mesh: dp: 1 (over z), tp: 32 (over y, x, core).
Axes of the slice: x: 4, y: 4, z: 1, core: 2. Of those that a mesh axis runs over, the one named last changes fastest.
The devices are a block of a 4x4x8 slice.
Arguments:
- token_ids: int32 [16384], P('dp')
- embed_table: bfloat16 [50304, 768], P('tp')
- norm_gain: bfloat16 [768], replicated
- w_in: bfloat16 [768, 3072], P(None, 'tp')
- w_out: bfloat16 [3072, 768], P('tp')
Outputs:
- output: bfloat16 [16384, 768], P(('dp', 'tp'))
All inputs are finite; a program needn't handle non-finite values.
Results may differ from a plain program's by a relative error of at most 0.00790572.
Values are sent between devices in bfloat16 or wider.
A program may use at most 768 MiB of HBM per device.

v0:
```python
import jax
import jax.numpy as jnp
from jax import lax
from jax.sharding import PartitionSpec as P

RMS_EPS = 1e-6


def rms_norm(row_vals, norm_gain):
    rows_f32 = row_vals.astype(jnp.float32)
    inv_rms = lax.rsqrt(jnp.mean(rows_f32 * rows_f32, axis=-1, keepdims=True) + RMS_EPS)
    return (rows_f32 * inv_rms * norm_gain.astype(jnp.float32)).astype(jnp.bfloat16)


def solution(mesh):
    def device_step(token_ids, table_shard, norm_gain, w_in_shard, w_out_shard):
        shard_rows = table_shard.shape[0]
        row_offset = lax.axis_index("tp") * shard_rows
        local_ids = token_ids - row_offset
        owned = (local_ids >= 0) & (local_ids < shard_rows)
        looked_up = jnp.take(table_shard, jnp.clip(local_ids, 0, shard_rows - 1), axis=0, mode="clip")
        partial_rows = jnp.where(owned[:, None], looked_up, jnp.zeros((), jnp.bfloat16))
        embedded = lax.psum_scatter(partial_rows, "tp", scatter_dimension=0, tiled=True)
        normed = rms_norm(embedded, norm_gain)
        normed_all = lax.all_gather(normed, "tp", axis=0, tiled=True)
        pre_act = jnp.dot(normed_all, w_in_shard, preferred_element_type=jnp.float32).astype(jnp.bfloat16)
        activated = jax.nn.gelu(pre_act.astype(jnp.float32), approximate=True).astype(jnp.bfloat16)
        mlp_part = jnp.dot(activated, w_out_shard, preferred_element_type=jnp.float32)
        mlp_sum = lax.psum_scatter(mlp_part, "tp", scatter_dimension=0, tiled=True)
        return (embedded.astype(jnp.float32) + mlp_sum).astype(jnp.bfloat16)

    return jax.shard_map(
        device_step,
        mesh=mesh,
        in_specs=(P("dp"), P("tp", None), P(), P(None, "tp"), P("tp", None)),
        out_specs=P(("dp", "tp"), None),
        check_vma=False,
    )
```

profile of v0, /device:TPU:97, one launch (start us, length us, event | category | flops | bytes accessed | tf_op | source)
XLA Modules:
  0.0 572.6 jit_solution(6287667069673520708)
XLA Ops:
  6.5 0.0 copy-start
  6.6 0.0 reduce-scatter.3.cloned.1.call-start
  6.6 1.0 compare_and_fusion
  7.6 0.9 clamp_clamp_fusion
  8.4 0.0 copy-done
  8.4 68.3 %gather_fusion = bf16[16384,768]{1,0:T(8,128)(2,1)} fusion(bf16[1572,768]{1,0:T(8,128)(2,1)S(1)} %copy-done, s32[16384]{0:T(1024)S(1)} %clamp_clamp_fusion), kind=kCustom, calls=%fused_computation | custom fusion | bytes 50397184 | tf_op jit(solution)/shard_map/jit(_take)/gather | solution.py:21
  76.7 23.4 %broadcast_select_fusion = bf16[16384,768]{1,0:T(8,128)(2,1)} fusion(bf16[16384,768]{1,0:T(8,128)(2,1)} %gather_fusion, pred[16384]{0:T(1024)(128)(4,1)S(1)} %compare_and_fusion), kind=kLoop, calls=%fused_computation.1 | loop fusion | flops 12582912 | bytes 50348032 | tf_op jit(solution)/shard_map/jit(_where)/select_n | solution.py:22
  100.1 0.0 copy-start.5
  100.1 0.0 copy-start.3
  100.1 0.0 copy-start.4
  100.1 0.1 reduce-scatter.3.cloned.1.call-update
  100.2 0.1 all-gather.2.cloned.1.call-start
  100.3 0.5 copy-done.5
  100.8 135.1 %reduce-scatter.3.cloned.1.call-done = bf16[512,768]{1,0:T(8,128)(2,1)} async-done(((bf16[16384,768]{1,0:T(8,128)(2,1)}), bf16[512,768]{1,0:T(8,128)(2,1)}) %reduce-scatter.3.cloned.1.call-update) | async-done | bytes 786448 | tf_op jit(solution)/shard_map/reduce_scatter | solution.py:23
  236.0 1.4 fusion.14
  237.3 2.3 fusion.16
  239.6 0.1 all-gather.2.cloned.1.call-update
  239.7 0.1 reduce-scatter.5.cloned.1.call-start
  239.7 87.1 %all-gather.2.cloned.1.call-done = bf16[16384,768]{1,0:T(8,128)(2,1)} async-done(((bf16[512,768]{1,0:T(8,128)(2,1)}), bf16[16384,768]{1,0:T(8,128)(2,1)}) %all-gather.2.cloned.1.call-update) | async-done | bytes 25165840 | tf_op jit(solution)/shard_map/all_gather | solution.py:25
  326.8 0.0 copy-done.3
  326.8 0.0 copy-done.4
  326.8 28.1 %fusion.9 = f32[16384,768]{1,0:T(8,128)} fusion(bf16[96,768]{1,0:T(8,128)(2,1)S(1)} %copy-done.4, bf16[16384,768]{1,0:T(8,128)(2,1)} %all-gather.2.cloned.1.call-done, bf16[768,96]{0,1:T(8,128)(2,1)S(1)} %copy-done.3), kind=kOutput, calls=%fused_computation.13 | convolution fusion | flops 4849139712 | bytes 75792384 | tf_op jit(solution)/shard_map/dot_general | solution.py:28
  355.0 0.0 copy-start.2
  355.0 0.1 reduce-scatter.5.cloned.1.call-update
  355.0 0.0 copy-start.1
  355.1 208.5 %reduce-scatter.5.cloned.1.call-done = f32[512,768]{1,0:T(8,128)} async-done(((f32[16384,768]{1,0:T(8,128)}), f32[512,768]{1,0:T(8,128)}) %reduce-scatter.5.cloned.1.call-update) | async-done | bytes 1572880 | tf_op jit(solution)/shard_map/reduce_scatter | solution.py:29
  563.6 0.0 copy-done.2
  563.6 2.5 fusion.17
  566.1 0.0 copy-done.1
  (2 shorter events, 0.0 us)
Async XLA Ops:
  6.5 1.9 copy-start
  6.6 229.4 %reduce-scatter.3.cloned.1.call-start = ((), (), s32[]{:S(2)}) async-start(), calls=%async_computation.2 | async-start | bytes 25952256 | tf_op jit(solution)/shard_map/reduce_scatter | solution.py:23
  100.1 0.7 copy-start.5
  100.1 226.7 %copy-start.3 = (bf16[768,96]{0,1:T(8,128)(2,1)S(1)}, bf16[768,96]{0,1:T(8,128)(2,1)}, u32[]{:S(2)}) copy-start(bf16[768,96]{0,1:T(8,128)(2,1)} %param.8) | copy-start | bytes 442372
  100.1 226.7 %copy-start.4 = (bf16[96,768]{1,0:T(8,128)(2,1)S(1)}, bf16[96,768]{1,0:T(8,128)(2,1)}, u32[]{:S(2)}) copy-start(bf16[96,768]{1,0:T(8,128)(2,1)} %param.9) | copy-start | bytes 442372
  100.2 226.6 %all-gather.2.cloned.1.call-start = ((), (), s32[]{:S(2)}) async-start(), calls=%async_computation.3 | async-start | bytes 25952256 | tf_op jit(solution)/shard_map/all_gather | solution.py:25
  239.7 323.9 %reduce-scatter.5.cloned.1.call-start = ((), (), s32[]{:S(2)}) async-start(), calls=%async_computation.4 | async-start | bytes 51904512 | tf_op jit(solution)/shard_map/reduce_scatter | solution.py:29
  355.0 208.6 %copy-start.2 = (bf16[512,768]{1,0:T(8,128)(2,1)S(1)}, bf16[512,768]{1,0:T(8,128)(2,1)}, u32[]{:S(2)}) copy-start(bf16[512,768]{1,0:T(8,128)(2,1)} %reduce-scatter.3.cloned.1.call-done) | copy-start | bytes 2359300
  355.0 211.0 %copy-start.1 = (bf16[1572,768]{1,0:T(8,128)(2,1)S(1)}, bf16[1572,768]{1,0:T(8,128)(2,1)}, u32[]{:S(2)}) copy-start(bf16[1572,768]{1,0:T(8,128)(2,1)} %param.6) | copy-start | bytes 7243780
Sparse Core Ops, SparseCore 0:
  100.3 135.5 reduce-scatter.2
  239.8 87.0 all-gather.1
  355.2 208.3 reduce-scatter.4
where the time goes:
time: 573 us
  waiting for transfers between devices  431 us (75%)
  local copies, waits for them, and re-layouts  68.8 us (12%)
  other arithmetic  31.4 us (5%)
  matrix products  28.1 us (5%)
  between operations  13.2 us (2%)
    reduce_scatter x1, waiting for transfers between devices, device_step(): mlp_sum = lax.psum_scatter(mlp_part, 'tp', scatter_dimension=0, tiled=True)  209 us
    reduce_scatter x1, waiting for transfers between devices, device_step(): lax.psum_scatter(partial_rows, 'tp', scatter_dimension=0, tiled=True)  135 us
    all_gather x1, waiting for transfers between devices, device_step(): normed_all = lax.all_gather(normed, 'tp', axis=0, tiled=True)  87.1 us
    gather x1, local copies, waits for them, and re-layouts, device_step(): jnp.take(table_shard, jnp.clip(local_ids, 0, shard_rows - 1), axis=0, mod...  68.3 us
    dot_general x1, matrix products, device_step(): jnp.dot(activated, w_out_shard, preferred_element_type=jnp.float32)  28.1 us
    select_n x1, other arithmetic, device_step(): jnp.where(owned[:, None], looked_up, jnp.zeros((), jnp.bfloat16))  23.4 us
  transfers between devices with their start and end apart: 3, of which 3 were waited for; matrix products, arithmetic and copies ran while one was open for 0% of the time, Pallas kernels for 0%

commit v1 on v0

v1 whole, which is shorter than its diff:
```python
import functools
import math

import jax
import jax.numpy as jnp
from jax import lax
from jax.experimental import pallas as pl
from jax.experimental.pallas import tpu as pltpu
from jax.sharding import PartitionSpec as P

RMS_EPS = 1e-6
MESH = pl.DeviceIdType.MESH
CAP = 80
GROUP = 8
F32, BF16 = jnp.float32, jnp.bfloat16


def iota(shape, dim):
    return lax.broadcasted_iota(jnp.int32, shape, dim).astype(F32)


def kernel(n, side, cap, do_rows, do_mlp, *refs):
    refs = list(refs)
    take = lambda count: [refs.pop(0) for _ in range(count)]
    if do_rows:
        round_ref, ids_ref, table_ref = take(3)
    else:
        (x_in_ref,) = take(1)
    if do_mlp:
        gain_ref, w_ref = take(2)
    (out_ref,) = take(1)
    if do_rows and do_mlp:
        (count_ref,) = take(1)
    x_ref, acc_ref, send_sem = take(3)
    if do_rows:
        key_ref, local_ref, hot_ref, pack_ref, rows_ref, rows_sem = take(6)
        vocab, tokens = table_ref.shape[0], ids_ref.shape[1]
    if do_mlp:
        w_all, w1_ref, w2_ref, n_ref, w_sem, sib_sem = take(6)

    me = lax.axis_index("tp")
    y, x, core = me // (2 * side), (me // 2) % side, me % 2

    def device(dy, dx, dc=0):
        return (lax.rem(y + dy + side, side) * side + lax.rem(x + dx + side, side)) * 2 + lax.rem(core + dc, 2)

    sent = []

    def send(src, dst, recv_sem, target):
        copy = pltpu.make_async_remote_copy(
            src_ref=src, dst_ref=dst, send_sem=send_sem.at[len(sent)], recv_sem=recv_sem,
            device_id={"tp": target}, device_id_type=MESH)
        copy.start()
        sent.append(copy)

    def wait(ref, recv_sem):
        pltpu.make_async_remote_copy(
            src_ref=ref, dst_ref=ref, send_sem=send_sem.at[0], recv_sem=recv_sem,
            device_id={"tp": me}, device_id_type=MESH).wait_recv()

    barrier = pltpu.get_barrier_semaphore()

    def greet(k, carry):
        pl.semaphore_signal(barrier, inc=1, device_id={"tp": lax.rem(me + k, n)}, device_id_type=MESH)
        return carry

    lax.fori_loop(1, n, greet, 0)

    def piece(half, a, b, owner_core):
        dx, dy = (a, b) if half == 0 else (b, a)
        return w_all.at[lax.rem(y - dy + side, side), lax.rem(x - dx + side, side), owner_core, half]

    def along(half, first, step):
        return device(0, step) if (half == 0) == first else device(step, 0)

    def spot(a, b):
        return a * side + b

    def second_axis(half, a, src, dst):
        send(src, dst, w_sem.at[half, 0, spot(a, 1)], along(half, False, 1))
        send(src, dst, w_sem.at[half, 0, spot(a, 3)], along(half, False, -1))

    def own_weights(half):
        src, dst = w_ref.at[half], piece(half, 0, 0, core)
        send(src, dst, w_sem.at[half, 0, spot(1, 0)], along(half, True, 1))
        send(src, dst, w_sem.at[half, 0, spot(3, 0)], along(half, True, -1))
        second_axis(half, 0, src, dst)
        send(src, dst, sib_sem.at[half, spot(0, 0)], device(0, 0, 1))

    def got(half, a, b):
        here = piece(half, a, b, core)
        if b == 2 or (a, b) == (2, 0):
            for part in range(2):
                wait(here.at[part], w_sem.at[half, part, spot(a, b)])
        else:
            wait(here, w_sem.at[half, 0, spot(a, b)])
        if b == 0:
            if a == 1:
                send(here.at[0], here.at[0], w_sem.at[half, 0, spot(2, 0)], along(half, True, 1))
            if a == 3:
                send(here.at[1], here.at[1], w_sem.at[half, 1, spot(2, 0)], along(half, True, -1))
            second_axis(half, a, here, here)
        if b == 1:
            send(here.at[0], here.at[0], w_sem.at[half, 0, spot(a, 2)], along(half, False, 1))
        if b == 3:
            send(here.at[1], here.at[1], w_sem.at[half, 1, spot(a, 2)], along(half, False, -1))
        send(here, here, sib_sem.at[half, spot(a, b)], device(0, 0, 1))

    def sibling(b):
        for half in range(2):
            for a in range(side):
                wait(piece(half, a, b, 1 - core), sib_sem.at[half, spot(a, b)])

    if do_rows:
        ids = ids_ref[...].astype(F32)
        local = ids - (me * vocab).astype(F32)
        owned = (local >= 0) & (local < vocab)
        before = (iota((tokens, tokens), 0) < iota((tokens, tokens), 1)).astype(BF16)
        rank = jnp.dot(jnp.where(owned, 1.0, 0.0).astype(BF16), before, preferred_element_type=F32)
        first = (round_ref[0] * cap).astype(F32)
        key_ref[...] = jnp.where(owned, rank - first, -1.0)
        local_ref[...] = local + 1.0

    if do_mlp:
        w_all[y, x, core] = w_ref[...]

    pl.semaphore_wait(barrier, n - 1)

    if do_mlp:
        own_weights(0)
        own_weights(1)

    if do_rows:
        def pack(group):
            for j in range(GROUP):
                dest = lax.rem(me + group * GROUP + j, n)
                key, val = key_ref[pl.ds(dest, 1), :], local_ref[pl.ds(dest, 1), :]
                row = jnp.sum(jnp.where(key == iota((cap, tokens), 0), val, 0.0), axis=1, keepdims=True) - 1.0
                hot_ref[j] = (row == iota((cap, vocab), 1)).astype(BF16)
            rows = jnp.dot(hot_ref[...].reshape(GROUP * cap, vocab), table_ref[...], preferred_element_type=F32)
            pack_ref[pl.ds(group * GROUP, GROUP)] = rows.astype(BF16).reshape(GROUP, cap, -1)

        def send_rows(group):
            for k in range(max(1, group * GROUP), (group + 1) * GROUP):
                send(pack_ref.at[k], rows_ref.at[me], rows_sem.at[k], lax.rem(me + k, n))

        for group in range(n // GROUP):
            pack(group)
            if group == 0:
                rows_ref[me] = pack_ref[0]
            else:
                send_rows(group - 1)
            if do_mlp and group == 1:
                for half in range(2):
                    got(half, 1, 0)
                    got(half, 3, 0)
            if do_mlp and group == 2:
                for half in range(2):
                    got(half, 0, 1)
                    got(half, 0, 3)
        if do_mlp:
            for half in range(2):
                got(half, 2, 0)
        send_rows(n // GROUP - 1)

        mine = ids_ref[pl.ds(me, 1), :].astype(F32)
        owner_row = jnp.floor((mine + 0.5) * (1.0 / vocab))
        p_col, p_row = iota((tokens, tokens), 0), iota((tokens, tokens), 1)
        owner_col = jnp.sum(jnp.where(p_col == p_row, owner_row, 0.0), axis=1, keepdims=True)
        place = jnp.sum(jnp.where((owner_col == owner_row) & (p_row < p_col), 1.0, 0.0), axis=1, keepdims=True)
        place = place - first
        slot = jnp.where((place >= 0) & (place < cap), owner_col * cap + place, -1.0)
        if do_mlp:
            owner_all = jnp.floor((ids + 0.5) * (1.0 / vocab))
            most = jnp.zeros((n, 1), F32)
            for owner in range(n):
                most = jnp.maximum(most, jnp.sum(jnp.where(owner_all == owner, 1.0, 0.0), axis=1, keepdims=True))
            count_ref[...] = jnp.broadcast_to(jnp.max(most, axis=0, keepdims=True), count_ref.shape)

        for k in range(1, n):
            wait(rows_ref.at[lax.rem(me - k + n, n)], rows_sem.at[k])
        for group in range(n // GROUP):
            hot = (slot - (group * GROUP * cap) == iota((tokens, GROUP * cap), 1)).astype(BF16)
            part = jnp.dot(hot, rows_ref[pl.ds(group * GROUP, GROUP)].reshape(GROUP * cap, -1),
                           preferred_element_type=F32)
            if group == 0:
                acc_ref[...] = part
            else:
                acc_ref[...] += part
        x_ref[...] = acc_ref[...].astype(BF16)
    else:
        x_ref[...] = x_in_ref[...]
        for half in range(2):
            got(half, 1, 0)
            got(half, 3, 0)
            got(half, 0, 1)
            got(half, 0, 3)
            got(half, 2, 0)

    if do_mlp:
        rows = x_ref[...].astype(F32)
        inv_rms = lax.rsqrt(jnp.mean(rows * rows, axis=-1, keepdims=True) + RMS_EPS)
        n_ref[...] = (rows * inv_rms * gain_ref[...].astype(F32)).astype(BF16)
        acc_ref[...] = jnp.zeros_like(acc_ref)
        span = w1_ref.shape[0] // 2
        tile = min(256, acc_ref.shape[0])

        def mlp(b):
            row, col = lax.rem(y - b + side, side), lax.rem(x - b + side, side)
            for part, dst in enumerate((w1_ref, w2_ref)):
                dst[:span] = w_all[row, :, :, 0, part].reshape(span, -1)
                dst[span:] = w_all[:, col, :, 1, part].reshape(span, -1)

            def step(t, carry):
                at = pl.ds(pl.multiple_of(t * tile, tile), tile)
                u = lax.dot_general(n_ref[at, :], w1_ref[...], (((1,), (1,)), ((), ())), preferred_element_type=F32)
                h = jax.nn.gelu(u.astype(BF16).astype(F32), approximate=True).astype(BF16)
                acc_ref[at, :] += jnp.dot(h, w2_ref[...], preferred_element_type=F32)
                return carry

            lax.fori_loop(0, acc_ref.shape[0] // tile, step, 0)

        sibling(0)
        mlp(0)
        for a in (1, 3, 2):
            for half in range(2):
                got(half, a, 1)
                got(half, a, 3)
        sibling(1)
        mlp(1)
        for a in (0, 1, 3, 2):
            for half in range(2):
                got(half, a, 2)
        sibling(3)
        mlp(3)
        sibling(2)
        mlp(2)
        out_ref[...] = (x_ref[...].astype(F32) + acc_ref[...]).astype(BF16)
    else:
        out_ref[...] = x_ref[...]
    for copy in sent:
        copy.wait_send()


def call(n, side, cap, do_rows, do_mlp, tokens, dim, vocab, share):
    vmem, dma = pltpu.VMEM, pltpu.SemaphoreType.DMA
    spec = pl.BlockSpec(memory_space=pltpu.VMEM)
    in_specs, out_shape, sends = [], [jax.ShapeDtypeStruct((tokens, dim), BF16)], 0
    scratch = []
    if do_rows:
        in_specs += [pl.BlockSpec(memory_space=pltpu.SMEM), spec, spec]
        scratch += [vmem((n, tokens), F32), vmem((n, tokens), F32), vmem((GROUP, cap, vocab), BF16),
                    vmem((n, cap, dim), BF16), vmem((n, cap, dim), BF16), dma((n,))]
        sends += n - 1
    else:
        in_specs += [spec]
    if do_mlp:
        in_specs += [spec, spec]
        scratch += [vmem((side, side, 2, 2, 2, share // 2, dim), BF16), vmem((n * share // side, dim), BF16),
                    vmem((n * share // side, dim), BF16), vmem((tokens, dim), BF16),
                    dma((2, 2, side * side)), dma((2, side * side))]
        sends += 2 * (4 + 16 + side * side)
    if do_rows and do_mlp:
        out_shape += [jax.ShapeDtypeStruct((8, 128), F32)]
    scratch = [vmem((tokens, dim), BF16), vmem((tokens, dim), F32), dma((sends,))] + scratch
    return pl.pallas_call(
        functools.partial(kernel, n, side, cap, do_rows, do_mlp),
        out_shape=out_shape,
        in_specs=in_specs,
        out_specs=[spec] * len(out_shape),
        scratch_shapes=scratch,
        compiler_params=pltpu.CompilerParams(
            collective_id=2 * do_rows + do_mlp, has_side_effects=True, vmem_limit_bytes=60 * 2**20),
    )


def solution(mesh):
    n = mesh.shape["tp"]
    side = math.isqrt(n // 2)

    def device_step(token_ids, table_shard, norm_gain, w_in_shard, w_out_shard):
        vocab, dim = table_shard.shape
        share = w_out_shard.shape[0]
        tokens = token_ids.shape[0] // n
        make = functools.partial(call, n, side, CAP, tokens=tokens, dim=dim, vocab=vocab, share=share)
        ids = token_ids.reshape(n, tokens)
        gain = norm_gain.reshape(1, dim)
        weights = jnp.stack([w_in_shard.T.reshape(2, share // 2, dim), w_out_shard.reshape(2, share // 2, dim)], axis=1)
        out, most = make(True, True)(jnp.zeros((1,), jnp.int32), ids, table_shard, gain, weights)
        rounds = lax.div(most[0, 0].astype(jnp.int32) + CAP - 1, CAP)

        def more_rounds():
            def one(carry):
                r, rows = carry
                (new,) = make(True, False)(r.reshape(1), ids, table_shard)
                return r + 1, rows + new

            _, rows = lax.while_loop(lambda carry: carry[0] < rounds, one,
                                     (jnp.int32(0), jnp.zeros((tokens, dim), BF16)))
            return make(False, True)(rows, gain, weights)[0]

        return lax.cond(rounds > 1, more_rounds, lambda: out)

    return jax.shard_map(
        device_step,
        mesh=mesh,
        in_specs=(P("dp"), P("tp", None), P(), P(None, "tp"), P("tp", None)),
        out_specs=P(("dp", "tp"), None),
        check_vma=False,
    )
```

time: 573 us -> 121 us (0.21)
  waiting for transfers between devices: 431 us -> 0 us
  Pallas kernels: 0 us -> 113 us
  local copies, waits for them, and re-layouts: 68.8 us -> 4.95 us
  other arithmetic: 31.4 us -> 1.02 us
  matrix products: 28.1 us -> 0 us
  between operations: 13.2 us -> 0.69 us
    reduce_scatter x2 -> x0, waiting for transfers between devices: 344 us -> none  [the longest x1 209 us: device_step(): mlp_sum = lax.psum_scatter(mlp_part, 'tp', scatter_dimension=0, tiled=True)]
    pallas_call x0 -> x1, Pallas kernels: none -> 113 us  [device_step(): make(True, True)]
    all_gather x1 -> x0, waiting for transfers between devices: 87.1 us -> none  [device_step(): normed_all = lax.all_gather(normed, 'tp', axis=0, tiled=True)]
    gather x1 -> x0, local copies, waits for them, and re-layouts: 68.3 us -> none  [device_step(): jnp.take(table_shard, jnp.clip(local_ids, 0, shard_rows - 1), axis=0, mod...]
    dot_general x1 -> x0, matrix products: 28.1 us -> none  [device_step(): jnp.dot(activated, w_out_shard, preferred_element_type=jnp.float32)]
    select_n x1 -> x0, other arithmetic: 23.4 us -> none  [device_step(): jnp.where(owned[:, None], looked_up, jnp.zeros((), jnp.bfloat16))]
  transfers between devices with their start and end apart: 3 -> 0, of which waited for: 3 -> 0; matrix products, arithmetic and copies ran while one was open for 0% -> 0% of each run, Pallas kernels for 0% -> 0%
where the time goes in v1:
time: 121 us; the launch traced here: 120 us
  Pallas kernels  113 us (93%)
  local copies, waits for them, and re-layouts  4.95 us (4%)
    pallas_call x1, Pallas kernels, device_step(): make(True, True)  113 us

profile of v1, /device:TPU:97, one launch (start us, length us, event | category | flops | bytes accessed | tf_op | source)
XLA Modules:
  0.0 120.4 jit_solution(3981932861985423171)
XLA Ops:
  0.0 0.0 copy-start
  0.0 0.8 reshape.15.refs_3_
  0.8 0.9 reshape.14.refs_1_
  1.7 1.0 pad_maximum_fusion.refs_4_
  2.7 113.4 %shard_map.57 = (bf16[512,768]{1,0:T(8,128)(2,1)}, f32[8,128]{1,0:T(8,128)}) custom-call(s32[1]{0:T(128)} %constant.13.clone.1.refs_0_, s32[32,512]{1,0:T(8,128)S(1)} %reshape.14.refs_1_, bf16[1572,768]{1,0:T(8,128)(2,1)} %refs_2_.1, bf16[1,768]{1,0:T(2,128)(2,1)S(1)} %reshape.15.refs_3_, bf16[2,2,48,768]{3,2,1,0:T(8,128)(2,1)S(1)} %pad_maximum_fusion.refs_4_), custom_call_target="tpu_custom_call" | custom-call | tf_op jit(solution)/shard_map/pallas_call | solution.py:289
  116.2 1.2 slice.3
  118.0 0.0 copy-done
  118.0 0.3 conditional.1
  118.3 2.1 %copy.19 = bf16[512,768]{1,0:T(8,128)(2,1)} copy(bf16[512,768]{1,0:T(8,128)(2,1)} %get-tuple-element.56) | data formatting | bytes 1572864
Async XLA Ops:
  0.0 118.0 %copy-start = (bf16[1572,768]{1,0:T(8,128)(2,1)S(1)}, bf16[1572,768]{1,0:T(8,128)(2,1)}, u32[]{:S(2)}) copy-start(bf16[1572,768]{1,0:T(8,128)(2,1)} %refs_2_.1) | copy-start | bytes 7243780

commit v2 on v0

v2 whole, which is shorter than its diff:
```python
import functools
import math

import jax
import jax.numpy as jnp
from jax import lax
from jax.experimental import pallas as pl
from jax.experimental.pallas import tpu as pltpu
from jax.sharding import PartitionSpec as P

RMS_EPS = 1e-6
MESH = pl.DeviceIdType.MESH
TURN_CAP, LAST_CAP = 224, 272
CAP, GROUP = 64, 8
F32, BF16 = jnp.float32, jnp.bfloat16


def iota(shape, dim):
    return lax.broadcasted_iota(jnp.int32, shape, dim).astype(F32)


def ones(mask):
    return jnp.where(mask, 1.0, 0.0)


def count_before(mask):
    tokens = mask.shape[1]
    before = ones(iota((tokens, tokens), 0) < iota((tokens, tokens), 1)).astype(BF16)
    return jnp.dot(mask.astype(BF16), before, preferred_element_type=F32)


def as_column(row):
    tokens = row.shape[1]
    return jnp.sum(jnp.where(iota((tokens, tokens), 0) == iota((tokens, tokens), 1), row, 0.0), axis=1, keepdims=True)


def place_among(kind):
    column = as_column(kind)
    tokens = kind.shape[1]
    same = (column == kind) & (iota((tokens, tokens), 1) < iota((tokens, tokens), 0))
    return column, jnp.sum(ones(same), axis=1, keepdims=True)


def coords(device, side):
    y = jnp.floor((device + 0.5) * (0.5 / side))
    x = jnp.floor((device - y * (2 * side) + 0.5) * 0.5)
    return y, x, device - y * (2 * side) - x * 2


def owner_of(ids, vocab):
    return jnp.floor((ids + 0.5) * (1.0 / vocab))


def greet_all(n, me):
    def greet(k, carry):
        pl.semaphore_signal(pltpu.get_barrier_semaphore(), inc=1, device_id={"tp": lax.rem(me + k, n)},
                            device_id_type=MESH)
        return carry

    lax.fori_loop(1, n, greet, 0)


def remote(src, dst, send_sem, recv_sem, target):
    return pltpu.make_async_remote_copy(src_ref=src, dst_ref=dst, send_sem=send_sem, recv_sem=recv_sem,
                                        device_id={"tp": target}, device_id_type=MESH)


def rows_kernel(n, cap, round_ref, ids_ref, table_ref, out_ref, key_ref, local_ref, hot_ref, pack_ref, rows_ref, acc_ref,
                send_sem, rows_sem):
    vocab, tokens = table_ref.shape[0], ids_ref.shape[1]
    me = lax.axis_index("tp")
    greet_all(n, me)
    local = ids_ref[...].astype(F32) - (me * vocab).astype(F32)
    owned = (local >= 0) & (local < vocab)
    first = (round_ref[0] * cap).astype(F32)
    key_ref[...] = jnp.where(owned, count_before(ones(owned)) - first, -1.0)
    local_ref[...] = local + 1.0
    pl.semaphore_wait(pltpu.get_barrier_semaphore(), n - 1)

    def pack(group, carry):
        def fill(j, carry):
            dest = lax.rem(me + group * GROUP + j, n)
            key, val = key_ref[pl.ds(dest, 1), :], local_ref[pl.ds(dest, 1), :]
            row = jnp.sum(jnp.where(key == iota((cap, tokens), 0), val, 0.0), axis=1, keepdims=True) - 1.0
            hot_ref[j] = (row == iota((cap, vocab), 1)).astype(BF16)
            return carry

        lax.fori_loop(0, GROUP, fill, 0)
        rows = jnp.dot(hot_ref[...].reshape(GROUP * cap, vocab), table_ref[...], preferred_element_type=F32)
        pack_ref[pl.ds(group * GROUP, GROUP)] = rows.astype(BF16).reshape(GROUP, cap, -1)
        return carry

    lax.fori_loop(0, n // GROUP, pack, 0)

    def pair(k, source):
        return remote(pack_ref.at[k], rows_ref.at[source], send_sem.at[k], rows_sem.at[k], lax.rem(me + k, n))

    def start(k, carry):
        pair(k, me).start()
        return carry

    lax.fori_loop(1, n, start, 0)
    rows_ref[me] = pack_ref[0]
    owner, place = place_among(owner_of(ids_ref[pl.ds(me, 1), :].astype(F32), vocab))
    place = place - first
    slot = jnp.where((place >= 0) & (place < cap), owner * cap + place, -1.0)

    def finish(k, carry):
        pair(k, lax.rem(me - k + n, n)).wait_recv()
        pair(k, me).wait_send()
        return carry

    lax.fori_loop(1, n, finish, 0)
    acc_ref[...] = jnp.zeros_like(acc_ref)

    def unpack(group, carry):
        hot = (slot - (group * (GROUP * cap)).astype(F32) == iota((tokens, GROUP * cap), 1)).astype(BF16)
        acc_ref[...] += jnp.dot(hot, rows_ref[pl.ds(group * GROUP, GROUP)].reshape(GROUP * cap, -1),
                                preferred_element_type=F32)
        return carry

    lax.fori_loop(0, n // GROUP, unpack, 0)
    out_ref[...] = acc_ref[...].astype(BF16)


def block_kernel(n, side, do_rows, *refs):
    refs = list(refs)
    take = lambda count: [refs.pop(0) for _ in range(count)]
    if do_rows:
        ids_ref, table_ref = take(2)
    else:
        (x_in_ref,) = take(1)
    gain_ref, w_ref, out_ref = take(3)
    if do_rows:
        (count_ref,) = take(1)
    x_ref, acc_ref, w_all, w1_ref, w2_ref, n_ref, send_sem, w_sem, sib_sem = take(9)
    if do_rows:
        key_ref, local_ref, owner_ref, hot_ref, pack_ref, mid_ref, turn_ref, last_ref, rows_ref, mid_sem, rows_sem = take(11)
        vocab, tokens = table_ref.shape[0], ids_ref.shape[1]

    me = lax.axis_index("tp")
    y, x, core = me // (2 * side), (me // 2) % side, me % 2

    def device(dy, dx, dc=0):
        return (lax.rem(y + dy + side, side) * side + lax.rem(x + dx + side, side)) * 2 + lax.rem(core + dc, 2)

    sent = []

    def send(src, dst, recv_sem, target):
        copy = remote(src, dst, send_sem.at[len(sent)], recv_sem, target)
        copy.start()
        sent.append(copy)

    def wait(ref, recv_sem):
        remote(ref, ref, send_sem.at[0], recv_sem, me).wait_recv()

    greet_all(n, me)

    def piece(half, a, b, owner_core):
        dx, dy = (a, b) if half == 0 else (b, a)
        return w_all.at[lax.rem(y - dy + side, side), lax.rem(x - dx + side, side), owner_core, half]

    def along(half, first, step):
        return device(0, step) if (half == 0) == first else device(step, 0)

    def spot(a, b):
        return a * side + b

    def second_axis(half, a, src, dst):
        send(src, dst, w_sem.at[half, 0, spot(a, 1)], along(half, False, 1))
        send(src, dst, w_sem.at[half, 0, spot(a, 3)], along(half, False, -1))

    def own_weights(half):
        src, dst = w_ref.at[half], piece(half, 0, 0, core)
        send(src, dst, w_sem.at[half, 0, spot(1, 0)], along(half, True, 1))
        send(src, dst, w_sem.at[half, 0, spot(3, 0)], along(half, True, -1))
        second_axis(half, 0, src, dst)
        send(src, dst, sib_sem.at[half, spot(0, 0)], device(0, 0, 1))

    def got(half, a, b):
        here = piece(half, a, b, core)
        if b == 2 or (a, b) == (2, 0):
            for part in range(2):
                wait(here.at[part], w_sem.at[half, part, spot(a, b)])
        else:
            wait(here, w_sem.at[half, 0, spot(a, b)])
        if b == 0:
            if a == 1:
                send(here.at[0], here.at[0], w_sem.at[half, 0, spot(2, 0)], along(half, True, 1))
            if a == 3:
                send(here.at[1], here.at[1], w_sem.at[half, 1, spot(2, 0)], along(half, True, -1))
            second_axis(half, a, here, here)
        if b == 1:
            send(here.at[0], here.at[0], w_sem.at[half, 0, spot(a, 2)], along(half, False, 1))
        if b == 3:
            send(here.at[1], here.at[1], w_sem.at[half, 1, spot(a, 2)], along(half, False, -1))
        send(here, here, sib_sem.at[half, spot(a, b)], device(0, 0, 1))

    def got_all(*spots):
        for a, b in spots:
            for half in range(2):
                got(half, a, b)

    def sibling(b):
        for half in range(2):
            for a in range(side):
                wait(piece(half, a, b, 1 - core), sib_sem.at[half, spot(a, b)])

    def line_device(half, line, i):
        in_x, in_y = (i * side + line) * 2, (line * side + i) * 2 + 1
        return in_x if isinstance(half, int) and half == 0 else in_y if isinstance(half, int) else jnp.where(half == 0, in_x, in_y)

    w_all[y, x, core] = w_ref[...]
    if do_rows:
        ids = ids_ref[...].astype(F32)
        local = ids - (me * vocab).astype(F32)
        owned = ones((local >= 0) & (local < vocab))
        dy, dx, dc = coords(iota((n, n), 0), side)
        ey, ex, ec = coords(iota((n, n), 1), side)
        same_line = ones(dc == ec) * jnp.where(dc == 0, ones(dx == ex), ones(dy == ey))
        earlier = same_line * jnp.where(dc == 0, ones(ey < dy), ones(ex < dx))
        in_line = jnp.dot(earlier.astype(BF16), owned.astype(BF16), preferred_element_type=F32)
        rank = count_before(owned) + jnp.sum(in_line, axis=1, keepdims=True)
        key_ref[...] = jnp.where(owned > 0, rank, -1.0)
        local_ref[...] = local + 1.0
        owner_ref[...] = owner_of(ids, vocab)

    pl.semaphore_wait(pltpu.get_barrier_semaphore(), n - 1)
    own_weights(0)
    own_weights(1)

    if do_rows:
        first_axis = jnp.where(core == 0, x, y)
        last_axis = jnp.where(core == 0, y, x)
        turn_cap, last_cap = mid_ref.shape[1], rows_ref.shape[1]

        def pack(half, line):
            row = jnp.zeros((turn_cap, 1), F32)
            for i in range(side):
                dest = line_device(half, line, i)
                key, val = key_ref[pl.ds(dest, 1), :], local_ref[pl.ds(dest, 1), :]
                row += jnp.sum(jnp.where(key == iota((turn_cap, tokens), 0), val, 0.0), axis=1, keepdims=True)
            hot_ref[...] = (row - 1.0 == iota((turn_cap, vocab), 1)).astype(BF16)
            return jnp.dot(hot_ref[...], table_ref[...], preferred_element_type=F32).astype(BF16)

        todo = []
        for step in (1, 3, 2):
            for half in range(2):
                at = len(todo)
                here = x if half == 0 else y
                pack_ref[at] = pack(half, lax.rem(here + step, side))
                target = (y * side + lax.rem(x + step, side)) * 2 if half == 0 else (lax.rem(y + step, side) * side + x) * 2 + 1
                todo.append((at, here * 2 + core, mid_sem.at[step * 2 + core], target))
                if at > 0:
                    at, j, sem, target = todo[at - 1]
                    send(pack_ref.at[at], mid_ref.at[j], sem, target)
        at = len(todo)
        pack_ref[at] = pack(1 - core, last_axis)
        send(pack_ref.at[at - 1], mid_ref.at[todo[-1][1]], todo[-1][2], todo[-1][3])
        mid_ref[first_axis * 2 + core] = pack(core, first_axis)
        send(pack_ref.at[at], mid_ref.at[last_axis * 2 + core], mid_sem.at[0], device(0, 0, 1))
        got_all((1, 0), (3, 0))

        j = lax.broadcasted_iota(jnp.int32, (2 * side, 1), 0)
        source = jnp.where(core == 0, y * (2 * side) + j, (j >> 1) * (2 * side) + x * 2 + (j & 1)).astype(F32)
        for i in range(side):
            mine = owner_ref[pl.ds(line_device(core, first_axis, i), 1), :]
            turn_ref[i * 2 * side:(i + 1) * 2 * side, :] = ones(mine == source)
        from_source = turn_ref[...]
        in_block = count_before(from_source)
        r, c = iota((n, n), 0), iota((n, n), 1)
        (ri, _, _), (ci, _, _) = coords(r, side), coords(c, side)
        earlier = (r - ri * (2 * side) == c - ci * (2 * side)) & (ci < ri)
        in_line = jnp.dot(ones(earlier).astype(BF16), from_source.astype(BF16), preferred_element_type=F32)
        slot = in_block + jnp.sum(in_line, axis=1, keepdims=True) + 1.0
        for i in range(side):
            part = slice(i * 2 * side, (i + 1) * 2 * side)
            mask = from_source[part]
            at = jnp.sum(mask * (slot[part] + j.astype(F32) * turn_cap), axis=0, keepdims=True)
            rank = jnp.sum(in_block[part], axis=0, keepdims=True)
            key_ref[i:i + 1, :] = jnp.where(at > 0, rank, -1.0)
            local_ref[i:i + 1, :] = at

        own_y, own_x, _ = coords(owner_ref[pl.ds(me, 1), :], side)
        via, place = place_among(jnp.where(core == 0, own_y, own_x))
        slot = via * last_cap + place

        def count(owner, counts):
            here = jnp.sum(ones(owner_ref[...] == owner.astype(F32)), axis=1, keepdims=True)
            return jnp.where(iota(counts.shape, 1) == owner.astype(F32), here, counts)

        counts = lax.fori_loop(0, n, count, jnp.zeros((n, 128), F32))
        exact = functools.partial(jnp.dot, precision=lax.Precision.HIGHEST, preferred_element_type=F32)
        bundles = exact(same_line, counts)
        oy, ox, _ = coords(iota((128, 128), 0), side)
        g = iota((128, 128), 1)
        blocks = exact(counts, ones((oy == g) | ((oy < side) & (ox == g - side))))
        lane = iota((n, 128), 1)
        dest_core = coords(iota((n, 128), 0), side)[2]
        counted = jnp.where(dest_core == 0, ones(lane < side), ones((lane >= side) & (lane < 2 * side)))
        over = ones(bundles > turn_cap) + counted * ones(blocks > last_cap)
        worst = lambda value: jnp.max(jnp.max(value, axis=0, keepdims=True), axis=1, keepdims=True)
        count_ref[0:1, :] = jnp.broadcast_to(worst(over), (1, 128))
        count_ref[1:2, :] = jnp.broadcast_to(worst(counts), (1, 128))

        wait(mid_ref.at[first_axis * 2 + 1 - core], mid_sem.at[0])
        for step in (1, 3, 2):
            for sc in range(2):
                wait(mid_ref.at[lax.rem(first_axis - step + side, side) * 2 + sc], mid_sem.at[step * 2 + sc])

        def turn(step):
            i = lax.rem(last_axis + step, side)
            key, val = key_ref[pl.ds(i, 1), :], local_ref[pl.ds(i, 1), :]
            row = jnp.sum(jnp.where(key == iota((last_cap, tokens), 0), val, 0.0), axis=1, keepdims=True) - 1.0
            hot = (row == iota((last_cap, 2 * side * turn_cap), 1)).astype(BF16)
            return jnp.dot(hot, mid_ref[...].reshape(2 * side * turn_cap, -1), preferred_element_type=F32).astype(BF16)

        def send_turn(step):
            send(last_ref.at[step], rows_ref.at[last_axis], rows_sem.at[step],
                 jnp.where(core == 0, device(step, 0), device(0, step)))

        last_ref[1] = turn(1)
        last_ref[3] = turn(3)
        send_turn(1)
        last_ref[2] = turn(2)
        send_turn(3)
        rows_ref[last_axis] = turn(0)
        send_turn(2)
        got_all((2, 0), (0, 1), (0, 3), (1, 1), (1, 3), (3, 1), (3, 3))

        for step in (1, 3, 2):
            wait(rows_ref.at[lax.rem(last_axis - step + side, side)], rows_sem.at[step])
        hot = (slot == iota((tokens, side * last_cap), 1)).astype(BF16)
        x_ref[...] = jnp.dot(hot, rows_ref[...].reshape(side * last_cap, -1), preferred_element_type=F32).astype(BF16)
    else:
        x_ref[...] = x_in_ref[...]
        got_all((1, 0), (3, 0), (2, 0), (0, 1), (0, 3), (1, 1), (1, 3), (3, 1), (3, 3))

    rows = x_ref[...].astype(F32)
    inv_rms = lax.rsqrt(jnp.mean(rows * rows, axis=-1, keepdims=True) + RMS_EPS)
    n_ref[...] = (rows * inv_rms * gain_ref[...].astype(F32)).astype(BF16)
    acc_ref[...] = jnp.zeros_like(acc_ref)
    span = w1_ref.shape[0] // 2
    tile = min(256, acc_ref.shape[0])

    def mlp(b):
        row, col = lax.rem(y - b + side, side), lax.rem(x - b + side, side)
        for part, dst in enumerate((w1_ref, w2_ref)):
            dst[:span] = w_all[row, :, :, 0, part].reshape(span, -1)
            dst[span:] = w_all[:, col, :, 1, part].reshape(span, -1)

        def step(t, carry):
            at = pl.ds(pl.multiple_of(t * tile, tile), tile)
            u = lax.dot_general(n_ref[at, :], w1_ref[...], (((1,), (1,)), ((), ())), preferred_element_type=F32)
            h = jax.nn.gelu(u.astype(BF16).astype(F32), approximate=True).astype(BF16)
            acc_ref[at, :] += jnp.dot(h, w2_ref[...], preferred_element_type=F32)
            return carry

        lax.fori_loop(0, acc_ref.shape[0] // tile, step, 0)

    if do_rows:
        sibling(0)
        mlp(0)
        got_all((2, 1), (2, 3))
        sibling(1)
        mlp(1)
        got_all((0, 2), (1, 2), (3, 2))
        sibling(3)
        mlp(3)
        got_all((2, 2))
        sibling(2)
        mlp(2)
    else:
        got_all((2, 1), (2, 3), (0, 2), (1, 2), (3, 2), (2, 2))
        for b in range(side):
            sibling(b)

        def every(b, carry):
            mlp(b)
            return carry

        lax.fori_loop(0, side, every, 0)
    out_ref[...] = (x_ref[...].astype(F32) + acc_ref[...]).astype(BF16)
    for copy in sent:
        copy.wait_send()


def params(collective_id):
    return pltpu.CompilerParams(collective_id=collective_id, has_side_effects=True, vmem_limit_bytes=60 * 2**20)


def rows_call(n, tokens, dim, vocab):
    vmem, dma = pltpu.VMEM, pltpu.SemaphoreType.DMA
    spec = pl.BlockSpec(memory_space=pltpu.VMEM)
    return pl.pallas_call(
        functools.partial(rows_kernel, n, CAP),
        out_shape=jax.ShapeDtypeStruct((tokens, dim), BF16),
        in_specs=[pl.BlockSpec(memory_space=pltpu.SMEM), spec, spec],
        out_specs=spec,
        scratch_shapes=[vmem((n, tokens), F32), vmem((n, tokens), F32), vmem((GROUP, CAP, vocab), BF16),
                        vmem((n, CAP, dim), BF16), vmem((n, CAP, dim), BF16), vmem((tokens, dim), F32),
                        dma((n,)), dma((n,))],
        compiler_params=params(0))


def block_call(n, side, do_rows, tokens, dim, vocab, share):
    vmem, dma = pltpu.VMEM, pltpu.SemaphoreType.DMA
    spec = pl.BlockSpec(memory_space=pltpu.VMEM)
    out_shape = [jax.ShapeDtypeStruct((tokens, dim), BF16)]
    sends = 2 * (4 + 16 + side * side) + (7 + 3 if do_rows else 0)
    scratch = [vmem((tokens, dim), BF16), vmem((tokens, dim), F32),
               vmem((side, side, 2, 2, 2, share // 2, dim), BF16), vmem((n * share // side, dim), BF16),
               vmem((n * share // side, dim), BF16), vmem((tokens, dim), BF16),
               dma((sends,)), dma((2, 2, side * side)), dma((2, side * side))]
    if do_rows:
        out_shape += [jax.ShapeDtypeStruct((2, 128), F32)]
        scratch += [vmem((n, tokens), F32)] * 3 + [
            vmem((TURN_CAP, vocab), BF16), vmem((2 * side - 1, TURN_CAP, dim), BF16), vmem((2 * side, TURN_CAP, dim), BF16),
            vmem((n, tokens), F32), vmem((side, LAST_CAP, dim), BF16), vmem((side, LAST_CAP, dim), BF16),
            dma((2 * side,)), dma((side,))]
    return pl.pallas_call(
        functools.partial(block_kernel, n, side, do_rows),
        out_shape=out_shape,
        in_specs=[spec] * (4 if do_rows else 3),
        out_specs=[spec] * len(out_shape),
        scratch_shapes=scratch,
        compiler_params=params(1 + do_rows))


def solution(mesh):
    n = mesh.shape["tp"]
    side = math.isqrt(n // 2)

    def device_step(token_ids, table_shard, norm_gain, w_in_shard, w_out_shard):
        vocab, dim = table_shard.shape
        share = w_out_shard.shape[0]
        tokens = token_ids.shape[0] // n
        ids = token_ids.reshape(n, tokens)
        gain = norm_gain.reshape(1, dim)
        weights = jnp.stack([w_in_shard.T.reshape(2, share // 2, dim), w_out_shard.reshape(2, share // 2, dim)], axis=1)
        out, counts = block_call(n, side, True, tokens, dim, vocab, share)(ids, table_shard, gain, weights)

        def in_rounds():
            rounds = lax.div(counts[1, 0].astype(jnp.int32) + CAP - 1, CAP)

            def one(carry):
                r, rows = carry
                return r + 1, rows + rows_call(n, tokens, dim, vocab)(r.reshape(1), ids, table_shard)

            _, rows = lax.while_loop(lambda carry: carry[0] < rounds, one,
                                     (jnp.int32(0), jnp.zeros((tokens, dim), BF16)))
            return block_call(n, side, False, tokens, dim, vocab, share)(rows, gain, weights)[0]

        return lax.cond(counts[0, 0] > 0, in_rounds, lambda: out)

    return jax.shard_map(
        device_step,
        mesh=mesh,
        in_specs=(P("dp"), P("tp", None), P(), P(None, "tp"), P("tp", None)),
        out_specs=P(("dp", "tp"), None),
        check_vma=False,
    )
```

time: 573 us -> 77.2 us (0.13)
  waiting for transfers between devices: 431 us -> 0 us
  Pallas kernels: 0 us -> 70 us
  local copies, waits for them, and re-layouts: 68.8 us -> 4.32 us
  other arithmetic: 31.4 us -> 1.73 us
  matrix products: 28.1 us -> 0 us
  between operations: 13.2 us -> 0.66 us
    reduce_scatter x2 -> x0, waiting for transfers between devices: 344 us -> none  [the longest x1 209 us: device_step(): mlp_sum = lax.psum_scatter(mlp_part, 'tp', scatter_dimension=0, tiled=True)]
    all_gather x1 -> x0, waiting for transfers between devices: 87.1 us -> none  [device_step(): normed_all = lax.all_gather(normed, 'tp', axis=0, tiled=True)]
    pallas_call x0 -> x1, Pallas kernels: none -> 70 us  [device_step(): block_call(n, side, True, tokens, dim, vocab, share)]
    gather x1 -> x0, local copies, waits for them, and re-layouts: 68.3 us -> none  [device_step(): jnp.take(table_shard, jnp.clip(local_ids, 0, shard_rows - 1), axis=0, mod...]
    dot_general x1 -> x0, matrix products: 28.1 us -> none  [device_step(): jnp.dot(activated, w_out_shard, preferred_element_type=jnp.float32)]
    select_n x1 -> x0, other arithmetic: 23.4 us -> none  [device_step(): jnp.where(owned[:, None], looked_up, jnp.zeros((), jnp.bfloat16))]
  transfers between devices with their start and end apart: 3 -> 0, of which waited for: 3 -> 0; matrix products, arithmetic and copies ran while one was open for 0% -> 0% of each run, Pallas kernels for 0% -> 0%
where the time goes in v2:
time: 77.2 us; the launch traced here: 77 us
  Pallas kernels  70 us (91%)
  local copies, waits for them, and re-layouts  4.32 us (6%)
  other arithmetic  1.73 us (2%)
    pallas_call x1, Pallas kernels, device_step(): block_call(n, side, True, tokens, dim, vocab, share)  70 us
    unnamed x3, local copies, waits for them, and re-layouts  2.07 us
    another operation x1, other arithmetic, device_step(): jnp.stack([w_in_shard.T.reshape(2, share // 2, dim), w_out_shard.reshape(...  1.73 us

profile of v2, /device:TPU:97, one launch (start us, length us, event | category | flops | bytes accessed | tf_op | source)
XLA Modules:
  0.0 77.0 jit_solution(4060302267873012622)
XLA Ops:
  0.0 0.0 copy-start
  0.0 0.8 %reshape.17.refs_2_ = bf16[1,768]{1,0:T(2,128)(2,1)S(1)} reshape(bf16[768]{0:T(1024)(128)(2,1)} %param.11) | data formatting | bytes 3072 | tf_op jit(solution)/shard_map/reshape | solution.py:439
  0.8 0.9 %reshape.16.refs_0_ = s32[32,512]{1,0:T(8,128)S(1)} reshape(s32[16384]{0:T(1024)} %param.9) | data formatting | bytes 131072 | tf_op jit(solution)/shard_map/reshape | solution.py:438
  1.7 1.7 %pad_maximum_fusion.refs_3_ = bf16[2,2,48,768]{3,2,1,0:T(8,128)(2,1)} fusion(bf16[2,1,48,768]{3,2,1,0:T(8,128)(2,1)} %bitcast.9, bf16[2,1,48,768]{3,2,1,0:T(8,128)(2,1)} %bitcast.10), kind=kLoop, calls=%fused_computation | loop fusion | flops 147456 | bytes 589824 | tf_op jit(solution)/shard_map/stack | solution.py:440
  3.4 70.0 %shard_map.57 = (bf16[512,768]{1,0:T(8,128)(2,1)}, f32[2,128]{1,0:T(2,128)S(1)}) custom-call(s32[32,512]{1,0:T(8,128)S(1)} %reshape.16.refs_0_, bf16[1572,768]{1,0:T(8,128)(2,1)} %refs_1_.1, bf16[1,768]{1,0:T(2,128)(2,1)S(1)} %reshape.17.refs_2_, bf16[2,2,48,768]{3,2,1,0:T(8,128)(2,1)} %pad_maximum_fusion.refs_3_), custom_call_target="tpu_custom_call" | custom-call | tf_op jit(solution)/shard_map/pallas_call | solution.py:441
  73.4 0.6 slice.6
  74.6 0.0 copy-done
  74.6 0.3 conditional.1
  74.9 2.1 %copy.19 = bf16[512,768]{1,0:T(8,128)(2,1)} copy(bf16[512,768]{1,0:T(8,128)(2,1)} %get-tuple-element.56) | data formatting | bytes 1572864
Async XLA Ops:
  0.0 74.6 %copy-start = (bf16[1572,768]{1,0:T(8,128)(2,1)S(1)}, bf16[1572,768]{1,0:T(8,128)(2,1)}, u32[]{:S(2)}) copy-start(bf16[1572,768]{1,0:T(8,128)(2,1)} %refs_1_.1) | copy-start | bytes 7243780

commit v3 on v2

--- a/solution.py
+++ b/solution.py
@@ -12,6 +12,8 @@
 MESH = pl.DeviceIdType.MESH
 TURN_CAP, LAST_CAP = 224, 272
 CAP, GROUP = 64, 8
+VMEM_LIMIT = 44 * 2**20
+GELU_SCALE = math.sqrt(2.0 / math.pi)
 F32, BF16 = jnp.float32, jnp.bfloat16
 
 
@@ -49,6 +51,15 @@
 
 def owner_of(ids, vocab):
     return jnp.floor((ids + 0.5) * (1.0 / vocab))
+
+
+def gelu(z):
+    return (0.5 * z) * (1.0 + jnp.tanh(z * (GELU_SCALE + GELU_SCALE * 0.044715 * (z * z))))
+
+
+def by_destination(ids_ref, n):
+    each = ids_ref.shape[0] // n
+    return jnp.concatenate([ids_ref[pl.ds(j, n, stride=each), :] for j in range(each)], axis=1).astype(F32)
 
 
 def greet_all(n, me):
@@ -127,16 +138,17 @@
     refs = list(refs)
     take = lambda count: [refs.pop(0) for _ in range(count)]
     if do_rows:
-        ids_ref, table_ref = take(2)
+        ids_in, table_in = take(2)
     else:
         (x_in_ref,) = take(1)
-    gain_ref, w_ref, out_ref = take(3)
-    if do_rows:
-        (count_ref,) = take(1)
-    x_ref, acc_ref, w_all, w1_ref, w2_ref, n_ref, send_sem, w_sem, sib_sem = take(9)
-    if do_rows:
-        key_ref, local_ref, owner_ref, hot_ref, pack_ref, mid_ref, turn_ref, last_ref, rows_ref, mid_sem, rows_sem = take(11)
-        vocab, tokens = table_ref.shape[0], ids_ref.shape[1]
+    gain_in, w1_in, w2_in, out_ref = take(4)
+    if do_rows:
+        over_ref, worst_ref = take(2)
+    gain_ref, x_ref, acc_ref, w_all, w1_ref, w2_ref, n_ref, send_sem, w_sem, sib_sem, in_sem = take(11)
+    if do_rows:
+        (ids_ref, table_ref, key_ref, local_ref, owner_ref, hot_ref, pack_ref, mid_ref, turn_ref, last_ref, rows_ref,
+         mid_sem, rows_sem) = take(13)
+        vocab, tokens = table_ref.shape[0], key_ref.shape[1]
 
     me = lax.axis_index("tp")
     y, x, core = me // (2 * side), (me // 2) % side, me % 2
@@ -155,6 +167,15 @@
         remote(ref, ref, send_sem.at[0], recv_sem, me).wait_recv()
 
     greet_all(n, me)
+    inputs = [pltpu.make_async_copy(part_in, w_all.at[y, x, core, :, part], in_sem.at[part])
+              for part, part_in in enumerate((w1_in, w2_in))]
+    inputs += [pltpu.make_async_copy(gain_in, gain_ref, in_sem.at[2])]
+    if do_rows:
+        inputs += [pltpu.make_async_copy(ids_in, ids_ref, in_sem.at[3]),
+                   pltpu.make_async_copy(table_in, table_ref, in_sem.at[4])]
+        inputs[3].start()
+    for copy in inputs[:3] + inputs[4:]:
+        copy.start()
 
     def piece(half, a, b, owner_core):
         dx, dy = (a, b) if half == 0 else (b, a)
@@ -166,16 +187,14 @@
     def spot(a, b):
         return a * side + b
 
-    def second_axis(half, a, src, dst):
-        send(src, dst, w_sem.at[half, 0, spot(a, 1)], along(half, False, 1))
-        send(src, dst, w_sem.at[half, 0, spot(a, 3)], along(half, False, -1))
-
-    def own_weights(half):
-        src, dst = w_ref.at[half], piece(half, 0, 0, core)
-        send(src, dst, w_sem.at[half, 0, spot(1, 0)], along(half, True, 1))
-        send(src, dst, w_sem.at[half, 0, spot(3, 0)], along(half, True, -1))
-        second_axis(half, 0, src, dst)
-        send(src, dst, sib_sem.at[half, spot(0, 0)], device(0, 0, 1))
+    def second_axis(half, a):
+        here = piece(half, a, 0, core)
+        send(here, here, w_sem.at[half, 0, spot(a, 1)], along(half, False, 1))
+        send(here, here, w_sem.at[half, 0, spot(a, 3)], along(half, False, -1))
+
+    def to_sibling(half, a, b):
+        here = piece(half, a, b, core)
+        send(here, here, sib_sem.at[half, spot(a, b)], device(0, 0, 1))
 
     def got(half, a, b):
         here = piece(half, a, b, core)
@@ -184,23 +203,26 @@
                 wait(here.at[part], w_sem.at[half, part, spot(a, b)])
         else:
             wait(here, w_sem.at[half, 0, spot(a, b)])
-        if b == 0:
-            if a == 1:
-                send(here.at[0], here.at[0], w_sem.at[half, 0, spot(2, 0)], along(half, True, 1))
-            if a == 3:
-                send(here.at[1], here.at[1], w_sem.at[half, 1, spot(2, 0)], along(half, True, -1))
-            second_axis(half, a, here, here)
+        if (a, b) == (1, 0):
+            send(here.at[0], here.at[0], w_sem.at[half, 0, spot(2, 0)], along(half, True, 1))
+        if (a, b) == (3, 0):
+            send(here.at[1], here.at[1], w_sem.at[half, 1, spot(2, 0)], along(half, True, -1))
         if b == 1:
             send(here.at[0], here.at[0], w_sem.at[half, 0, spot(a, 2)], along(half, False, 1))
         if b == 3:
             send(here.at[1], here.at[1], w_sem.at[half, 1, spot(a, 2)], along(half, False, -1))
-        send(here, here, sib_sem.at[half, spot(a, b)], device(0, 0, 1))
+        to_sibling(half, a, b)
 
     def got_all(*spots):
         for a, b in spots:
             for half in range(2):
                 got(half, a, b)
 
+    def spread(*firsts):
+        for a in firsts:
+            for half in range(2):
+                second_axis(half, a)
+
     def sibling(b):
         for half in range(2):
             for a in range(side):
@@ -210,9 +232,9 @@
         in_x, in_y = (i * side + line) * 2, (line * side + i) * 2 + 1
         return in_x if isinstance(half, int) and half == 0 else in_y if isinstance(half, int) else jnp.where(half == 0, in_x, in_y)
 
-    w_all[y, x, core] = w_ref[...]
-    if do_rows:
-        ids = ids_ref[...].astype(F32)
+    if do_rows:
+        inputs[3].wait()
+        ids = by_destination(ids_ref, n)
         local = ids - (me * vocab).astype(F32)
         owned = ones((local >= 0) & (local < vocab))
         dy, dx, dc = coords(iota((n, n), 0), side)
@@ -225,9 +247,17 @@
         local_ref[...] = local + 1.0
         owner_ref[...] = owner_of(ids, vocab)
 
+    inputs[0].wait()
+    inputs[1].wait()
     pl.semaphore_wait(pltpu.get_barrier_semaphore(), n - 1)
-    own_weights(0)
-    own_weights(1)
+    for half in range(2):
+        here = piece(half, 0, 0, core)
+        send(here, here, w_sem.at[half, 0, spot(1, 0)], along(half, True, 1))
+        send(here, here, w_sem.at[half, 0, spot(3, 0)], along(half, True, -1))
+    spread(0)
+    for half in range(2):
+        to_sibling(half, 0, 0)
+    inputs[2].wait()
 
     if do_rows:
         first_axis = jnp.where(core == 0, x, y)
@@ -243,6 +273,7 @@
             hot_ref[...] = (row - 1.0 == iota((turn_cap, vocab), 1)).astype(BF16)
             return jnp.dot(hot_ref[...], table_ref[...], preferred_element_type=F32).astype(BF16)
 
+        inputs[4].wait()
         todo = []
         for step in (1, 3, 2):
             for half in range(2):
@@ -254,12 +285,14 @@
                 if at > 0:
                     at, j, sem, target = todo[at - 1]
                     send(pack_ref.at[at], mid_ref.at[j], sem, target)
+            if step == 3:
+                got_all((1, 0), (3, 0))
         at = len(todo)
         pack_ref[at] = pack(1 - core, last_axis)
         send(pack_ref.at[at - 1], mid_ref.at[todo[-1][1]], todo[-1][2], todo[-1][3])
         mid_ref[first_axis * 2 + core] = pack(core, first_axis)
         send(pack_ref.at[at], mid_ref.at[last_axis * 2 + core], mid_sem.at[0], device(0, 0, 1))
-        got_all((1, 0), (3, 0))
+        spread(1)
 
         j = lax.broadcasted_iota(jnp.int32, (2 * side, 1), 0)
         source = jnp.where(core == 0, y * (2 * side) + j, (j >> 1) * (2 * side) + x * 2 + (j & 1)).astype(F32)
@@ -299,9 +332,8 @@
         dest_core = coords(iota((n, 128), 0), side)[2]
         counted = jnp.where(dest_core == 0, ones(lane < side), ones((lane >= side) & (lane < 2 * side)))
         over = ones(bundles > turn_cap) + counted * ones(blocks > last_cap)
-        worst = lambda value: jnp.max(jnp.max(value, axis=0, keepdims=True), axis=1, keepdims=True)
-        count_ref[0:1, :] = jnp.broadcast_to(worst(over), (1, 128))
-        count_ref[1:2, :] = jnp.broadcast_to(worst(counts), (1, 128))
+        over_ref[0] = jnp.max(over)
+        worst_ref[0] = jnp.max(counts)
 
         wait(mid_ref.at[first_axis * 2 + 1 - core], mid_sem.at[0])
         for step in (1, 3, 2):
@@ -326,7 +358,11 @@
         send_turn(3)
         rows_ref[last_axis] = turn(0)
         send_turn(2)
-        got_all((2, 0), (0, 1), (0, 3), (1, 1), (1, 3), (3, 1), (3, 3))
+        got_all((0, 1), (0, 3))
+        spread(3)
+        got_all((2, 0))
+        spread(2)
+        got_all((1, 1), (1, 3))
 
         for step in (1, 3, 2):
             wait(rows_ref.at[lax.rem(last_axis - step + side, side)], rows_sem.at[step])
@@ -334,26 +370,33 @@
         x_ref[...] = jnp.dot(hot, rows_ref[...].reshape(side * last_cap, -1), preferred_element_type=F32).astype(BF16)
     else:
         x_ref[...] = x_in_ref[...]
-        got_all((1, 0), (3, 0), (2, 0), (0, 1), (0, 3), (1, 1), (1, 3), (3, 1), (3, 3))
-
+        got_all((1, 0), (3, 0))
+        spread(1, 3)
+        got_all((2, 0))
+        spread(2)
+        got_all((0, 1), (0, 3), (1, 1), (1, 3), (3, 1), (3, 3), (2, 1), (2, 3), (0, 2), (1, 2), (3, 2), (2, 2))
+
+    gain = jnp.concatenate([gain_ref[i:i + 1, :] for i in range(gain_ref.shape[0])], axis=1).astype(F32)
     rows = x_ref[...].astype(F32)
     inv_rms = lax.rsqrt(jnp.mean(rows * rows, axis=-1, keepdims=True) + RMS_EPS)
-    n_ref[...] = (rows * inv_rms * gain_ref[...].astype(F32)).astype(BF16)
+    n_ref[...] = (rows * inv_rms * gain).astype(BF16)
     acc_ref[...] = jnp.zeros_like(acc_ref)
     span = w1_ref.shape[0] // 2
     tile = min(256, acc_ref.shape[0])
 
-    def mlp(b):
+    def mlp(b, owner_core=None):
         row, col = lax.rem(y - b + side, side), lax.rem(x - b + side, side)
+        cores = slice(None) if owner_core is None else pl.ds(owner_core, 1)
+        width = 2 * span if owner_core is None else span
         for part, dst in enumerate((w1_ref, w2_ref)):
-            dst[:span] = w_all[row, :, :, 0, part].reshape(span, -1)
-            dst[span:] = w_all[:, col, :, 1, part].reshape(span, -1)
+            dst[:width // 2] = w_all[row, :, cores, 0, part].reshape(width // 2, -1)
+            dst[width // 2:width] = w_all[:, col, cores, 1, part].reshape(width // 2, -1)
 
         def step(t, carry):
             at = pl.ds(pl.multiple_of(t * tile, tile), tile)
-            u = lax.dot_general(n_ref[at, :], w1_ref[...], (((1,), (1,)), ((), ())), preferred_element_type=F32)
-            h = jax.nn.gelu(u.astype(BF16).astype(F32), approximate=True).astype(BF16)
-            acc_ref[at, :] += jnp.dot(h, w2_ref[...], preferred_element_type=F32)
+            u = lax.dot_general(n_ref[at, :], w1_ref[:width], (((1,), (1,)), ((), ())), preferred_element_type=F32)
+            h = gelu(u.astype(BF16).astype(F32)).astype(BF16)
+            acc_ref[at, :] += jnp.dot(h, w2_ref[:width], preferred_element_type=F32)
             return carry
 
         lax.fori_loop(0, acc_ref.shape[0] // tile, step, 0)
@@ -361,17 +404,17 @@
     if do_rows:
         sibling(0)
         mlp(0)
-        got_all((2, 1), (2, 3))
+        got_all((3, 1), (3, 3), (2, 1), (2, 3))
         sibling(1)
         mlp(1)
-        got_all((0, 2), (1, 2), (3, 2))
+        got_all((0, 2), (1, 2))
         sibling(3)
         mlp(3)
-        got_all((2, 2))
+        got_all((3, 2), (2, 2))
+        mlp(2, core)
         sibling(2)
-        mlp(2)
+        mlp(2, 1 - core)
     else:
-        got_all((2, 1), (2, 3), (0, 2), (1, 2), (3, 2), (2, 2))
         for b in range(side):
             sibling(b)
 
@@ -386,7 +429,7 @@
 
 
 def params(collective_id):
-    return pltpu.CompilerParams(collective_id=collective_id, has_side_effects=True, vmem_limit_bytes=60 * 2**20)
+    return pltpu.CompilerParams(collective_id=collective_id, has_side_effects=True, vmem_limit_bytes=VMEM_LIMIT)
 
 
 def rows_call(n, tokens, dim, vocab):
@@ -405,24 +448,24 @@
 
 def block_call(n, side, do_rows, tokens, dim, vocab, share):
     vmem, dma = pltpu.VMEM, pltpu.SemaphoreType.DMA
-    spec = pl.BlockSpec(memory_space=pltpu.VMEM)
+    spec, hbm = pl.BlockSpec(memory_space=pltpu.VMEM), pl.BlockSpec(memory_space=pltpu.HBM)
     out_shape = [jax.ShapeDtypeStruct((tokens, dim), BF16)]
     sends = 2 * (4 + 16 + side * side) + (7 + 3 if do_rows else 0)
-    scratch = [vmem((tokens, dim), BF16), vmem((tokens, dim), F32),
+    scratch = [vmem((dim // 128, 128), BF16), vmem((tokens, dim), BF16), vmem((tokens, dim), F32),
                vmem((side, side, 2, 2, 2, share // 2, dim), BF16), vmem((n * share // side, dim), BF16),
                vmem((n * share // side, dim), BF16), vmem((tokens, dim), BF16),
-               dma((sends,)), dma((2, 2, side * side)), dma((2, side * side))]
-    if do_rows:
-        out_shape += [jax.ShapeDtypeStruct((2, 128), F32)]
-        scratch += [vmem((n, tokens), F32)] * 3 + [
+               dma((sends,)), dma((2, 2, side * side)), dma((2, side * side)), dma((5,))]
+    if do_rows:
+        out_shape += [jax.ShapeDtypeStruct((1,), F32)] * 2
+        scratch += [vmem((n * tokens // 128, 128), jnp.int32), vmem((vocab, dim), BF16)] + [vmem((n, tokens), F32)] * 3 + [
             vmem((TURN_CAP, vocab), BF16), vmem((2 * side - 1, TURN_CAP, dim), BF16), vmem((2 * side, TURN_CAP, dim), BF16),
             vmem((n, tokens), F32), vmem((side, LAST_CAP, dim), BF16), vmem((side, LAST_CAP, dim), BF16),
             dma((2 * side,)), dma((side,))]
     return pl.pallas_call(
         functools.partial(block_kernel, n, side, do_rows),
         out_shape=out_shape,
-        in_specs=[spec] * (4 if do_rows else 3),
-        out_specs=[spec] * len(out_shape),
+        in_specs=([hbm, hbm] if do_rows else [spec]) + [hbm] * 3,
+        out_specs=[spec] + [pl.BlockSpec(memory_space=pltpu.SMEM)] * (len(out_shape) - 1),
         scratch_shapes=scratch,
         compiler_params=params(1 + do_rows))
 
@@ -436,12 +479,13 @@
         share = w_out_shard.shape[0]
         tokens = token_ids.shape[0] // n
         ids = token_ids.reshape(n, tokens)
-        gain = norm_gain.reshape(1, dim)
-        weights = jnp.stack([w_in_shard.T.reshape(2, share // 2, dim), w_out_shard.reshape(2, share // 2, dim)], axis=1)
-        out, counts = block_call(n, side, True, tokens, dim, vocab, share)(ids, table_shard, gain, weights)
+        block = (norm_gain.reshape(dim // 128, 128), w_in_shard.T.reshape(2, share // 2, dim),
+                 w_out_shard.reshape(2, share // 2, dim))
+        out, over, worst = block_call(n, side, True, tokens, dim, vocab, share)(
+            token_ids.reshape(n * tokens // 128, 128), table_shard, *block)
 
         def in_rounds():
-            rounds = lax.div(counts[1, 0].astype(jnp.int32) + CAP - 1, CAP)
+            rounds = lax.div(worst[0].astype(jnp.int32) + CAP - 1, CAP)
 
             def one(carry):
                 r, rows = carry
@@ -449,9 +493,9 @@
 
             _, rows = lax.while_loop(lambda carry: carry[0] < rounds, one,
                                      (jnp.int32(0), jnp.zeros((tokens, dim), BF16)))
-            return block_call(n, side, False, tokens, dim, vocab, share)(rows, gain, weights)[0]
-
-        return lax.cond(counts[0, 0] > 0, in_rounds, lambda: out)
+            return block_call(n, side, False, tokens, dim, vocab, share)(rows, *block)[0]
+
+        return lax.cond(over[0] > 0, in_rounds, lambda: out)
 
     return jax.shard_map(
         device_step,

time: 77.2 us -> 71.1 us (0.921)
  local copies, waits for them, and re-layouts: 4.32 us -> 0.9 us
  other arithmetic: 1.73 us -> 0 us
  Pallas kernels: 70 us -> 69.1 us
    another operation x1 -> x0, other arithmetic: 1.73 us -> none  [device_step(): jnp.stack([w_in_shard.T.reshape(2, share // 2, dim), w_out_shard.reshape(...]
    reshape x2 -> x0, local copies, waits for them, and re-layouts: 1.69 us -> none  [the longest x1 0.85 us: device_step(): ids = token_ids.reshape(n, tokens)]
    unnamed x3 -> x9, local copies, waits for them, and re-layouts: 2.07 us -> 0.9 us
    pallas_call x1, Pallas kernels: 70 us -> 69.1 us  [device_step(): block_call(n, side, True, tokens, dim, vocab, share)]
where the time goes in v3:
time: 71.1 us; the launch traced here: 71 us
  Pallas kernels  69.1 us (97%)
  local copies, waits for them, and re-layouts  0.9 us (1%)
  between operations  0.74 us (1%)
    pallas_call x1, Pallas kernels, device_step(): block_call(n, side, True, tokens, dim, vocab, share)  69.1 us

profile of v3, /device:TPU:97, one launch (start us, length us, event | category | flops | bytes accessed | tf_op | source)
XLA Modules:
  0.0 71.0 jit_solution(2782569562870445632)
XLA Ops:
  0.0 0.0 copy-start
  0.0 0.0 copy-start.2
  0.0 0.0 copy-start.1
  0.0 0.0 copy-start.3
  0.0 69.1 %shard_map.57 = (bf16[512,768]{1,0:T(8,128)(2,1)S(1)}, f32[1]{0:T(128)}, f32[1]{0:T(128)}) custom-call(s32[128,128]{1,0:T(8,128)} %bitcast.15, bf16[1572,768]{1,0:T(8,128)(2,1)} %refs_1_.1, bf16[6,128]{1,0:T(8,128)(2,1)} %bitcast.16, bf16[2,48,768]{2,1,0:T(8,128)(2,1)} %bitcast.11, bf16[2,48,768]{2,1,0:T(8,128)(2,1)} %bitcast.13), custom_call_target="tpu_custom_call" | custom-call | tf_op jit(solution)/shard_map/pallas_call | solution.py:484
  69.8 0.0 copy-done
  69.8 0.0 copy-done.2
  69.8 0.0 copy-done.1
  69.8 0.0 copy-done.3
  69.8 0.3 conditional.1
  70.1 0.9 %copy.19 = bf16[512,768]{1,0:T(8,128)(2,1)} copy(bf16[512,768]{1,0:T(8,128)(2,1)S(1)} %get-tuple-element.62) | data formatting | bytes 1572864
Async XLA Ops:
  0.0 69.8 %copy-start = (bf16[1572,768]{1,0:T(8,128)(2,1)S(1)}, bf16[1572,768]{1,0:T(8,128)(2,1)}, u32[]{:S(2)}) copy-start(bf16[1572,768]{1,0:T(8,128)(2,1)} %refs_1_.1) | copy-start | bytes 7243780
  0.0 69.8 %copy-start.2 = (s32[16384]{0:T(1024)S(1)}, s32[16384]{0:T(1024)}, u32[]{:S(2)}) copy-start(s32[16384]{0:T(1024)} %param.9) | copy-start | bytes 196612
  0.0 69.8 %copy-start.1 = (bf16[768,96]{0,1:T(8,128)(2,1)S(1)}, bf16[768,96]{0,1:T(8,128)(2,1)}, u32[]{:S(2)}) copy-start(bf16[768,96]{0,1:T(8,128)(2,1)} %param.12) | copy-start | bytes 442372
  0.0 69.8 %copy-start.3 = (bf16[768]{0:T(1024)(128)(2,1)S(1)}, bf16[768]{0:T(1024)(128)(2,1)}, u32[]{:S(2)}) copy-start(bf16[768]{0:T(1024)(128)(2,1)} %param.11) | copy-start | bytes 4612

commit v4 on v3

--- a/solution.py
+++ b/solution.py
@@ -13,6 +13,8 @@
 TURN_CAP, LAST_CAP = 224, 272
 CAP, GROUP = 64, 8
 VMEM_LIMIT = 44 * 2**20
+DIRECT = (3,)
+EARLY = 2
 GELU_SCALE = math.sqrt(2.0 / math.pi)
 F32, BF16 = jnp.float32, jnp.bfloat16
 
@@ -166,7 +168,12 @@
     def wait(ref, recv_sem):
         remote(ref, ref, send_sem.at[0], recv_sem, me).wait_recv()
 
-    greet_all(n, me)
+    partners = [device(0, 0, 1)]
+    for step in (2, 1, 3):
+        for other in range(2):
+            partners += [device(0, step, other), device(step, 0, other)]
+    for partner in partners:
+        pl.semaphore_signal(pltpu.get_barrier_semaphore(), inc=1, device_id={"tp": partner}, device_id_type=MESH)
     inputs = [pltpu.make_async_copy(part_in, w_all.at[y, x, core, :, part], in_sem.at[part])
               for part, part_in in enumerate((w1_in, w2_in))]
     inputs += [pltpu.make_async_copy(gain_in, gain_ref, in_sem.at[2])]
@@ -189,6 +196,8 @@
 
     def second_axis(half, a):
         here = piece(half, a, 0, core)
+        if a in DIRECT:
+            send(here, here, w_sem.at[half, 0, spot(a, 2)], along(half, False, 2))
         send(here, here, w_sem.at[half, 0, spot(a, 1)], along(half, False, 1))
         send(here, here, w_sem.at[half, 0, spot(a, 3)], along(half, False, -1))
 
@@ -198,7 +207,7 @@
 
     def got(half, a, b):
         here = piece(half, a, b, core)
-        if b == 2 or (a, b) == (2, 0):
+        if (b == 2 and a not in DIRECT) or (a, b) == (2, 0):
             for part in range(2):
                 wait(here.at[part], w_sem.at[half, part, spot(a, b)])
         else:
@@ -207,26 +216,29 @@
             send(here.at[0], here.at[0], w_sem.at[half, 0, spot(2, 0)], along(half, True, 1))
         if (a, b) == (3, 0):
             send(here.at[1], here.at[1], w_sem.at[half, 1, spot(2, 0)], along(half, True, -1))
-        if b == 1:
+        if b == 1 and a not in DIRECT:
             send(here.at[0], here.at[0], w_sem.at[half, 0, spot(a, 2)], along(half, False, 1))
-        if b == 3:
+        if b == 3 and a not in DIRECT:
             send(here.at[1], here.at[1], w_sem.at[half, 1, spot(a, 2)], along(half, False, -1))
         to_sibling(half, a, b)
 
-    def got_all(*spots):
-        for a, b in spots:
+    def parse(spots):
+        return [(int(a), int(b)) for a, b in spots.split()]
+
+    def got_all(spots):
+        for a, b in parse(spots):
             for half in range(2):
                 got(half, a, b)
+
+    def from_sibling(spots):
+        for a, b in parse(spots):
+            for half in range(2):
+                wait(piece(half, a, b, 1 - core), sib_sem.at[half, spot(a, b)])
 
     def spread(*firsts):
         for a in firsts:
             for half in range(2):
                 second_axis(half, a)
-
-    def sibling(b):
-        for half in range(2):
-            for a in range(side):
-                wait(piece(half, a, b, 1 - core), sib_sem.at[half, spot(a, b)])
 
     def line_device(half, line, i):
         in_x, in_y = (i * side + line) * 2, (line * side + i) * 2 + 1
@@ -247,17 +259,20 @@
         local_ref[...] = local + 1.0
         owner_ref[...] = owner_of(ids, vocab)
 
-    inputs[0].wait()
-    inputs[1].wait()
-    pl.semaphore_wait(pltpu.get_barrier_semaphore(), n - 1)
-    for half in range(2):
-        here = piece(half, 0, 0, core)
-        send(here, here, w_sem.at[half, 0, spot(1, 0)], along(half, True, 1))
-        send(here, here, w_sem.at[half, 0, spot(3, 0)], along(half, True, -1))
-    spread(0)
-    for half in range(2):
-        to_sibling(half, 0, 0)
-    inputs[2].wait()
+    def enter():
+        inputs[0].wait()
+        inputs[1].wait()
+        pl.semaphore_wait(pltpu.get_barrier_semaphore(), len(partners))
+        for half in range(2):
+            here = piece(half, 0, 0, core)
+            send(here, here, w_sem.at[half, 0, spot(1, 0)], along(half, True, 1))
+            send(here, here, w_sem.at[half, 0, spot(3, 0)], along(half, True, -1))
+
+    def own():
+        spread(0)
+        for half in range(2):
+            to_sibling(half, 0, 0)
+        inputs[2].wait()
 
     if do_rows:
         first_axis = jnp.where(core == 0, x, y)
@@ -274,25 +289,24 @@
             return jnp.dot(hot_ref[...], table_ref[...], preferred_element_type=F32).astype(BF16)
 
         inputs[4].wait()
-        todo = []
-        for step in (1, 3, 2):
+        bundles = []
+        for step in (2, 1, 3):
             for half in range(2):
-                at = len(todo)
-                here = x if half == 0 else y
+                at, here = len(bundles), (x, y)[half]
                 pack_ref[at] = pack(half, lax.rem(here + step, side))
-                target = (y * side + lax.rem(x + step, side)) * 2 if half == 0 else (lax.rem(y + step, side) * side + x) * 2 + 1
-                todo.append((at, here * 2 + core, mid_sem.at[step * 2 + core], target))
-                if at > 0:
-                    at, j, sem, target = todo[at - 1]
-                    send(pack_ref.at[at], mid_ref.at[j], sem, target)
-            if step == 3:
-                got_all((1, 0), (3, 0))
-        at = len(todo)
-        pack_ref[at] = pack(1 - core, last_axis)
-        send(pack_ref.at[at - 1], mid_ref.at[todo[-1][1]], todo[-1][2], todo[-1][3])
+                target = ((y * side + lax.rem(x + step, side)) * 2, (lax.rem(y + step, side) * side + x) * 2 + 1)[half]
+                bundles.append((pack_ref.at[at], mid_ref.at[here * 2 + core], mid_sem.at[step * 2 + core], target))
+                if at == EARLY:
+                    enter()
+                    for bundle in bundles[:-1]:
+                        send(*bundle)
+                elif at > EARLY:
+                    send(*bundles[-2])
+        pack_ref[len(bundles)] = pack(1 - core, last_axis)
+        send(*bundles[-1])
+        own()
         mid_ref[first_axis * 2 + core] = pack(core, first_axis)
-        send(pack_ref.at[at], mid_ref.at[last_axis * 2 + core], mid_sem.at[0], device(0, 0, 1))
-        spread(1)
+        send(pack_ref.at[len(bundles)], mid_ref.at[last_axis * 2 + core], mid_sem.at[0], device(0, 0, 1))
 
         j = lax.broadcasted_iota(jnp.int32, (2 * side, 1), 0)
         source = jnp.where(core == 0, y * (2 * side) + j, (j >> 1) * (2 * side) + x * 2 + (j & 1)).astype(F32)
@@ -324,17 +338,19 @@
 
         counts = lax.fori_loop(0, n, count, jnp.zeros((n, 128), F32))
         exact = functools.partial(jnp.dot, precision=lax.Precision.HIGHEST, preferred_element_type=F32)
-        bundles = exact(same_line, counts)
+        in_bundle = exact(same_line, counts)
         oy, ox, _ = coords(iota((128, 128), 0), side)
         g = iota((128, 128), 1)
         blocks = exact(counts, ones((oy == g) | ((oy < side) & (ox == g - side))))
         lane = iota((n, 128), 1)
         dest_core = coords(iota((n, 128), 0), side)[2]
         counted = jnp.where(dest_core == 0, ones(lane < side), ones((lane >= side) & (lane < 2 * side)))
-        over = ones(bundles > turn_cap) + counted * ones(blocks > last_cap)
+        over = ones(in_bundle > turn_cap) + counted * ones(blocks > last_cap)
         over_ref[0] = jnp.max(over)
         worst_ref[0] = jnp.max(counts)
 
+        got_all("10 30")
+        spread(1)
         wait(mid_ref.at[first_axis * 2 + 1 - core], mid_sem.at[0])
         for step in (1, 3, 2):
             for sc in range(2):
@@ -351,18 +367,17 @@
             send(last_ref.at[step], rows_ref.at[last_axis], rows_sem.at[step],
                  jnp.where(core == 0, device(step, 0), device(0, step)))
 
+        last_ref[2] = turn(2)
         last_ref[1] = turn(1)
+        send_turn(2)
         last_ref[3] = turn(3)
         send_turn(1)
-        last_ref[2] = turn(2)
+        rows_ref[last_axis] = turn(0)
         send_turn(3)
-        rows_ref[last_axis] = turn(0)
-        send_turn(2)
-        got_all((0, 1), (0, 3))
+        got_all("01 03 20")
+        spread(2)
+        got_all("11 13")
         spread(3)
-        got_all((2, 0))
-        spread(2)
-        got_all((1, 1), (1, 3))
 
         for step in (1, 3, 2):
             wait(rows_ref.at[lax.rem(last_axis - step + side, side)], rows_sem.at[step])
@@ -370,58 +385,60 @@
         x_ref[...] = jnp.dot(hot, rows_ref[...].reshape(side * last_cap, -1), preferred_element_type=F32).astype(BF16)
     else:
         x_ref[...] = x_in_ref[...]
-        got_all((1, 0), (3, 0))
+        enter()
+        own()
+        got_all("10 30")
         spread(1, 3)
-        got_all((2, 0))
+        got_all("20")
         spread(2)
-        got_all((0, 1), (0, 3), (1, 1), (1, 3), (3, 1), (3, 3), (2, 1), (2, 3), (0, 2), (1, 2), (3, 2), (2, 2))
+        for spots in ("01 03 11 13", "31 33 21 23", "02 12 32 22"):
+            got_all(spots)
 
     gain = jnp.concatenate([gain_ref[i:i + 1, :] for i in range(gain_ref.shape[0])], axis=1).astype(F32)
     rows = x_ref[...].astype(F32)
     inv_rms = lax.rsqrt(jnp.mean(rows * rows, axis=-1, keepdims=True) + RMS_EPS)
     n_ref[...] = (rows * inv_rms * gain).astype(BF16)
     acc_ref[...] = jnp.zeros_like(acc_ref)
-    span = w1_ref.shape[0] // 2
-    tile = min(256, acc_ref.shape[0])
-
-    def mlp(b, owner_core=None):
-        row, col = lax.rem(y - b + side, side), lax.rem(x - b + side, side)
+    span = 2 * w_all.shape[5]
+
+    def mlp(spots, owner_core=None):
+        spots = parse(spots) if isinstance(spots, str) else spots
         cores = slice(None) if owner_core is None else pl.ds(owner_core, 1)
-        width = 2 * span if owner_core is None else span
+        rows = span if owner_core is None else span // 2
+        width = 2 * len(spots) * rows
         for part, dst in enumerate((w1_ref, w2_ref)):
-            dst[:width // 2] = w_all[row, :, cores, 0, part].reshape(width // 2, -1)
-            dst[width // 2:width] = w_all[:, col, cores, 1, part].reshape(width // 2, -1)
-
-        def step(t, carry):
-            at = pl.ds(pl.multiple_of(t * tile, tile), tile)
-            u = lax.dot_general(n_ref[at, :], w1_ref[:width], (((1,), (1,)), ((), ())), preferred_element_type=F32)
-            h = gelu(u.astype(BF16).astype(F32)).astype(BF16)
-            acc_ref[at, :] += jnp.dot(h, w2_ref[:width], preferred_element_type=F32)
+            at = 0
+            for a, b in spots:
+                for dx, dy, half in ((a, b, 0), (b, a, 1)):
+                    row, col = lax.rem(y - dy + side, side), lax.rem(x - dx + side, side)
+                    dst[at:at + rows] = w_all[row, col, cores, half, part].reshape(rows, -1)
+                    at += rows
+
+        u = lax.dot_general(n_ref[...], w1_ref[:width], (((1,), (1,)), ((), ())), preferred_element_type=F32)
+        h = gelu(u.astype(BF16).astype(F32)).astype(BF16)
+        acc_ref[...] += jnp.dot(h, w2_ref[:width], preferred_element_type=F32)
+
+    if do_rows:
+        from_sibling("00 10 20 30")
+        mlp("00 10 20 30")
+        got_all("02 21 23")
+        from_sibling("01 03 11 13")
+        mlp("01 03 11 13")
+        got_all("12")
+        mlp("02 12 21 23", core)
+        from_sibling("02 21 23 12")
+        mlp("02 12 21 23", 1 - core)
+        got_all("31 33 32 22")
+        mlp("31 33 32 22", core)
+        from_sibling("31 33 32 22")
+        mlp("31 33 32 22", 1 - core)
+    else:
+        def every(a, carry):
+            mlp([(a, b) for b in range(side)])
             return carry
 
-        lax.fori_loop(0, acc_ref.shape[0] // tile, step, 0)
-
-    if do_rows:
-        sibling(0)
-        mlp(0)
-        got_all((3, 1), (3, 3), (2, 1), (2, 3))
-        sibling(1)
-        mlp(1)
-        got_all((0, 2), (1, 2))
-        sibling(3)
-        mlp(3)
-        got_all((3, 2), (2, 2))
-        mlp(2, core)
-        sibling(2)
-        mlp(2, 1 - core)
-    else:
-        for b in range(side):
-            sibling(b)
-
-        def every(b, carry):
-            mlp(b)
-            return carry
-
+        for spots in ("00 01 02 03", "10 11 12 13", "20 21 22 23", "30 31 32 33"):
+            from_sibling(spots)
         lax.fori_loop(0, side, every, 0)
     out_ref[...] = (x_ref[...].astype(F32) + acc_ref[...]).astype(BF16)
     for copy in sent:
@@ -450,7 +467,7 @@
     vmem, dma = pltpu.VMEM, pltpu.SemaphoreType.DMA
     spec, hbm = pl.BlockSpec(memory_space=pltpu.VMEM), pl.BlockSpec(memory_space=pltpu.HBM)
     out_shape = [jax.ShapeDtypeStruct((tokens, dim), BF16)]
-    sends = 2 * (4 + 16 + side * side) + (7 + 3 if do_rows else 0)
+    sends = 2 * (4 + 16 - len(DIRECT) + side * side) + (7 + 3 if do_rows else 0)
     scratch = [vmem((dim // 128, 128), BF16), vmem((tokens, dim), BF16), vmem((tokens, dim), F32),
                vmem((side, side, 2, 2, 2, share // 2, dim), BF16), vmem((n * share // side, dim), BF16),
                vmem((n * share // side, dim), BF16), vmem((tokens, dim), BF16),

time: 71.1 us -> 69.1 us (0.972)
  Pallas kernels: 69.1 us -> 67.1 us
    pallas_call x1, Pallas kernels: 69.1 us -> 67.1 us  [device_step(): block_call(n, side, True, tokens, dim, vocab, share)]
where the time goes in v4:
time: 69.1 us; the launch traced here: 69 us
  Pallas kernels  67.1 us (97%)
  local copies, waits for them, and re-layouts  0.9 us (1%)
  between operations  0.74 us (1%)
    pallas_call x1, Pallas kernels, device_step(): block_call(n, side, True, tokens, dim, vocab, share)  67.1 us

profile of v4, /device:TPU:97, one launch (start us, length us, event | category | flops | bytes accessed | tf_op | source)
XLA Modules:
  0.0 69.0 jit_solution(732033390000050105)
XLA Ops:
  0.0 0.0 copy-start
  0.0 0.0 copy-start.2
  0.0 0.0 copy-start.1
  0.0 0.0 copy-start.3
  0.0 67.1 %shard_map.57 = (bf16[512,768]{1,0:T(8,128)(2,1)S(1)}, f32[1]{0:T(128)}, f32[1]{0:T(128)}) custom-call(s32[128,128]{1,0:T(8,128)} %bitcast.15, bf16[1572,768]{1,0:T(8,128)(2,1)} %refs_1_.1, bf16[6,128]{1,0:T(8,128)(2,1)} %bitcast.16, bf16[2,48,768]{2,1,0:T(8,128)(2,1)} %bitcast.11, bf16[2,48,768]{2,1,0:T(8,128)(2,1)} %bitcast.13), custom_call_target="tpu_custom_call" | custom-call | tf_op jit(solution)/shard_map/pallas_call | solution.py:501
  67.8 0.0 copy-done
  67.8 0.0 copy-done.2
  67.8 0.0 copy-done.1
  67.8 0.0 copy-done.3
  67.9 0.3 conditional.1
  68.1 0.9 %copy.19 = bf16[512,768]{1,0:T(8,128)(2,1)} copy(bf16[512,768]{1,0:T(8,128)(2,1)S(1)} %get-tuple-element.62) | data formatting | bytes 1572864
Async XLA Ops:
  0.0 67.8 %copy-start = (bf16[1572,768]{1,0:T(8,128)(2,1)S(1)}, bf16[1572,768]{1,0:T(8,128)(2,1)}, u32[]{:S(2)}) copy-start(bf16[1572,768]{1,0:T(8,128)(2,1)} %refs_1_.1) | copy-start | bytes 7243780
  0.0 67.8 %copy-start.2 = (s32[16384]{0:T(1024)S(1)}, s32[16384]{0:T(1024)}, u32[]{:S(2)}) copy-start(s32[16384]{0:T(1024)} %param.9) | copy-start | bytes 196612
  0.0 67.8 %copy-start.1 = (bf16[768,96]{0,1:T(8,128)(2,1)S(1)}, bf16[768,96]{0,1:T(8,128)(2,1)}, u32[]{:S(2)}) copy-start(bf16[768,96]{0,1:T(8,128)(2,1)} %param.12) | copy-start | bytes 442372
  0.0 67.8 %copy-start.3 = (bf16[768]{0:T(1024)(128)(2,1)S(1)}, bf16[768]{0:T(1024)(128)(2,1)}, u32[]{:S(2)}) copy-start(bf16[768]{0:T(1024)(128)(2,1)} %param.11) | copy-start | bytes 4612

commit v5 on v4

--- a/solution.py
+++ b/solution.py
@@ -14,7 +14,6 @@
 CAP, GROUP = 64, 8
 VMEM_LIMIT = 44 * 2**20
 DIRECT = (3,)
-EARLY = 2
 GELU_SCALE = math.sqrt(2.0 / math.pi)
 F32, BF16 = jnp.float32, jnp.bfloat16
 
@@ -296,11 +295,9 @@
                 pack_ref[at] = pack(half, lax.rem(here + step, side))
                 target = ((y * side + lax.rem(x + step, side)) * 2, (lax.rem(y + step, side) * side + x) * 2 + 1)[half]
                 bundles.append((pack_ref.at[at], mid_ref.at[here * 2 + core], mid_sem.at[step * 2 + core], target))
-                if at == EARLY:
+                if at == 0:
                     enter()
-                    for bundle in bundles[:-1]:
-                        send(*bundle)
-                elif at > EARLY:
+                else:
                     send(*bundles[-2])
         pack_ref[len(bundles)] = pack(1 - core, last_axis)
         send(*bundles[-1])

time: 69.1 us -> 67.8 us (0.981)
  Pallas kernels: 67.1 us -> 65.8 us
    pallas_call x1, Pallas kernels: 67.1 us -> 65.8 us  [device_step(): block_call(n, side, True, tokens, dim, vocab, share)]
where the time goes in v5:
time: 67.8 us; the launch traced here: 67.7 us
  Pallas kernels  65.8 us (97%)
  local copies, waits for them, and re-layouts  0.9 us (1%)
  between operations  0.74 us (1%)
    pallas_call x1, Pallas kernels, device_step(): block_call(n, side, True, tokens, dim, vocab, share)  65.8 us

profile of v5, /device:TPU:97, one launch (start us, length us, event | category | flops | bytes accessed | tf_op | source)
XLA Modules:
  0.0 67.7 jit_solution(8643772087781854020)
XLA Ops:
  0.0 0.0 copy-start
  0.0 0.0 copy-start.2
  0.0 0.0 copy-start.1
  0.0 0.0 copy-start.3
  0.0 65.8 %shard_map.57 = (bf16[512,768]{1,0:T(8,128)(2,1)S(1)}, f32[1]{0:T(128)}, f32[1]{0:T(128)}) custom-call(s32[128,128]{1,0:T(8,128)} %bitcast.15, bf16[1572,768]{1,0:T(8,128)(2,1)} %refs_1_.1, bf16[6,128]{1,0:T(8,128)(2,1)} %bitcast.16, bf16[2,48,768]{2,1,0:T(8,128)(2,1)} %bitcast.11, bf16[2,48,768]{2,1,0:T(8,128)(2,1)} %bitcast.13), custom_call_target="tpu_custom_call" | custom-call | tf_op jit(solution)/shard_map/pallas_call | solution.py:498
  66.5 0.0 copy-done
  66.5 0.0 copy-done.2
  66.5 0.0 copy-done.1
  66.5 0.0 copy-done.3
  66.5 0.3 conditional.1
  66.8 0.9 %copy.19 = bf16[512,768]{1,0:T(8,128)(2,1)} copy(bf16[512,768]{1,0:T(8,128)(2,1)S(1)} %get-tuple-element.62) | data formatting | bytes 1572864
Async XLA Ops:
  0.0 66.5 %copy-start = (bf16[1572,768]{1,0:T(8,128)(2,1)S(1)}, bf16[1572,768]{1,0:T(8,128)(2,1)}, u32[]{:S(2)}) copy-start(bf16[1572,768]{1,0:T(8,128)(2,1)} %refs_1_.1) | copy-start | bytes 7243780
  0.0 66.5 %copy-start.2 = (s32[16384]{0:T(1024)S(1)}, s32[16384]{0:T(1024)}, u32[]{:S(2)}) copy-start(s32[16384]{0:T(1024)} %param.9) | copy-start | bytes 196612
  0.0 66.5 %copy-start.1 = (bf16[768,96]{0,1:T(8,128)(2,1)S(1)}, bf16[768,96]{0,1:T(8,128)(2,1)}, u32[]{:S(2)}) copy-start(bf16[768,96]{0,1:T(8,128)(2,1)} %param.12) | copy-start | bytes 442372
  0.0 66.5 %copy-start.3 = (bf16[768]{0:T(1024)(128)(2,1)S(1)}, bf16[768]{0:T(1024)(128)(2,1)}, u32[]{:S(2)}) copy-start(bf16[768]{0:T(1024)(128)(2,1)} %param.11) | copy-start | bytes 4612

commit v6 on v5

--- a/solution.py
+++ b/solution.py
@@ -395,10 +395,11 @@
     rows = x_ref[...].astype(F32)
     inv_rms = lax.rsqrt(jnp.mean(rows * rows, axis=-1, keepdims=True) + RMS_EPS)
     n_ref[...] = (rows * inv_rms * gain).astype(BF16)
-    acc_ref[...] = jnp.zeros_like(acc_ref)
+    if not do_rows:
+        acc_ref[...] = jnp.zeros_like(acc_ref)
     span = 2 * w_all.shape[5]
 
-    def mlp(spots, owner_core=None):
+    def mlp(spots, owner_core=None, first=False):
         spots = parse(spots) if isinstance(spots, str) else spots
         cores = slice(None) if owner_core is None else pl.ds(owner_core, 1)
         rows = span if owner_core is None else span // 2
@@ -413,11 +414,12 @@
 
         u = lax.dot_general(n_ref[...], w1_ref[:width], (((1,), (1,)), ((), ())), preferred_element_type=F32)
         h = gelu(u.astype(BF16).astype(F32)).astype(BF16)
-        acc_ref[...] += jnp.dot(h, w2_ref[:width], preferred_element_type=F32)
+        part = jnp.dot(h, w2_ref[:width], preferred_element_type=F32)
+        acc_ref[...] = part if first else acc_ref[...] + part
 
     if do_rows:
         from_sibling("00 10 20 30")
-        mlp("00 10 20 30")
+        mlp("00 10 20 30", first=True)
         got_all("02 21 23")
         from_sibling("01 03 11 13")
         mlp("01 03 11 13")

time: 67.8 us -> 67.7 us (level)
  no operation moved by 1% of the time
where the time goes in v6:
time: 67.7 us; the launch traced here: 67.6 us
  Pallas kernels  65.7 us (97%)
  local copies, waits for them, and re-layouts  0.9 us (1%)
  between operations  0.74 us (1%)
    pallas_call x1, Pallas kernels, device_step(): block_call(n, side, True, tokens, dim, vocab, share)  65.7 us

profile of v6, /device:TPU:97, one launch (start us, length us, event | category | flops | bytes accessed | tf_op | source)
XLA Modules:
  0.0 67.6 jit_solution(1954536092828274863)
XLA Ops:
  0.0 0.0 copy-start
  0.0 0.0 copy-start.2
  0.0 0.0 copy-start.1
  0.0 0.0 copy-start.3
  0.0 65.7 %shard_map.57 = (bf16[512,768]{1,0:T(8,128)(2,1)S(1)}, f32[1]{0:T(128)}, f32[1]{0:T(128)}) custom-call(s32[128,128]{1,0:T(8,128)} %bitcast.15, bf16[1572,768]{1,0:T(8,128)(2,1)} %refs_1_.1, bf16[6,128]{1,0:T(8,128)(2,1)} %bitcast.16, bf16[2,48,768]{2,1,0:T(8,128)(2,1)} %bitcast.11, bf16[2,48,768]{2,1,0:T(8,128)(2,1)} %bitcast.13), custom_call_target="tpu_custom_call" | custom-call | tf_op jit(solution)/shard_map/pallas_call | solution.py:500
  66.4 0.0 copy-done
  66.4 0.0 copy-done.2
  66.4 0.0 copy-done.1
  66.5 0.0 copy-done.3
  66.5 0.3 conditional.1
  66.7 0.9 %copy.19 = bf16[512,768]{1,0:T(8,128)(2,1)} copy(bf16[512,768]{1,0:T(8,128)(2,1)S(1)} %get-tuple-element.62) | data formatting | bytes 1572864
Async XLA Ops:
  0.0 66.4 %copy-start = (bf16[1572,768]{1,0:T(8,128)(2,1)S(1)}, bf16[1572,768]{1,0:T(8,128)(2,1)}, u32[]{:S(2)}) copy-start(bf16[1572,768]{1,0:T(8,128)(2,1)} %refs_1_.1) | copy-start | bytes 7243780
  0.0 66.4 %copy-start.2 = (s32[16384]{0:T(1024)S(1)}, s32[16384]{0:T(1024)}, u32[]{:S(2)}) copy-start(s32[16384]{0:T(1024)} %param.9) | copy-start | bytes 196612
  0.0 66.4 %copy-start.1 = (bf16[768,96]{0,1:T(8,128)(2,1)S(1)}, bf16[768,96]{0,1:T(8,128)(2,1)}, u32[]{:S(2)}) copy-start(bf16[768,96]{0,1:T(8,128)(2,1)} %param.12) | copy-start | bytes 442372
  0.0 66.4 %copy-start.3 = (bf16[768]{0:T(1024)(128)(2,1)S(1)}, bf16[768]{0:T(1024)(128)(2,1)}, u32[]{:S(2)}) copy-start(bf16[768]{0:T(1024)(128)(2,1)} %param.11) | copy-start | bytes 4612
